TPU v7x, 32 devices: a 4x4x1 block of a 4x4x8 slice. The times are simulated.
32 devices in a mesh: dp: 1 (over z), tp: 4 (over y), cp: 8 (over x, core).
Axes of the slice: x: 4, y: 4, z: 1, core: 2. Of those that a mesh axis runs over, the one named last changes fastest.
The devices are a block of a 4x4x8 slice.
Arguments:
- x: bfloat16 [8192, 5120], P(('dp', 'cp', 'tp'))
- pos: int32 [8192], P(('dp', 'cp', 'tp'))
- g1: bfloat16 [5120], replicated
- g2: bfloat16 [5120], replicated
- wq: bfloat16 [5120, 5120], P(None, 'tp')
- wk: bfloat16 [5120, 1024], P(None, 'tp')
- wv: bfloat16 [5120, 1024], P(None, 'tp')
- wo: bfloat16 [5120, 5120], P('tp')
- w1: bfloat16 [5120, 13824], P(None, 'tp')
- w3: bfloat16 [5120, 13824], P(None, 'tp')
- w2: bfloat16 [13824, 5120], P('tp')
Outputs:
- output: bfloat16 [8192, 5120], P(('dp', 'cp', 'tp'))
All inputs are finite; a program needn't handle non-finite values.
Results may differ from a plain program's by a relative error of at most 0.00970005.
Values are sent between devices in bfloat16 or wider.
A program may use at most 768 MiB of HBM per device.

v0:
```python
import math
import jax
import jax.numpy as jnp
from jax import lax
from jax.sharding import PartitionSpec as P, NamedSharding

DH = 128
EPS = 1e-5
THETA = 500000.0


def rms_norm(v, g):
    vf = v.astype(jnp.float32)
    inv = lax.rsqrt(jnp.mean(vf * vf, axis=-1, keepdims=True) + EPS)
    return (vf * inv * g.astype(jnp.float32)).astype(jnp.bfloat16)


def rope(y, p):
    half = DH // 2
    freq = 1.0 / (THETA ** (jnp.arange(0, DH, 2, dtype=jnp.float32) / DH))
    ang = p.astype(jnp.float32)[..., None] * freq
    c = jnp.cos(ang)[..., None, :]
    s = jnp.sin(ang)[..., None, :]
    y1 = y[..., :half]
    y2 = y[..., half:]
    return jnp.concatenate([y1 * c - y2 * s, y2 * c + y1 * s], axis=-1)


def attend(q, k, v, qpos, kpos):
    nq, hl, dh = q.shape
    hk = k.shape[1]
    grp = hl // hk
    qb = nq
    while qb % 2 == 0 and qb * hl > 1024:
        qb = qb // 2
    qr = q.reshape(nq // qb, qb, hk, grp, dh)
    pr = qpos.reshape(nq // qb, qb)
    scale = 1.0 / math.sqrt(dh)

    def blk(qp):
        qq, pp = qp
        s = jnp.einsum('qkgd,skd->kgqs', qq, k, preferred_element_type=jnp.float32) * scale
        s = jnp.where(kpos[None, None, None, :] <= pp[None, None, :, None], s, -1e30)
        e = jnp.exp(s - jnp.max(s, axis=-1, keepdims=True))
        w = (e / jnp.sum(e, axis=-1, keepdims=True)).astype(jnp.bfloat16)
        o = jnp.einsum('kgqs,skd->qkgd', w, v, preferred_element_type=jnp.float32)
        return o.astype(jnp.bfloat16)

    return lax.map(blk, (qr, pr)).reshape(nq, hl * dh)


def solution(mesh):
    tok = P(('dp', 'cp', 'tp'), None)
    col = P(None, 'tp')
    row = P('tp', None)

    def local(x, pos, g1, g2, wq, wk, wv, wo, w1, w3, w2):
        a = lax.all_gather(rms_norm(x, g1), 'tp', axis=0, tiled=True)
        pg = lax.all_gather(pos, 'tp', axis=0, tiled=True)
        nr = a.shape[0]
        q = rope(jnp.dot(a, wq, preferred_element_type=jnp.float32).reshape(nr, -1, DH), pg).astype(jnp.bfloat16)
        k = rope(jnp.dot(a, wk, preferred_element_type=jnp.float32).reshape(nr, -1, DH), pg).astype(jnp.bfloat16)
        v = jnp.dot(a, wv, preferred_element_type=jnp.float32).astype(jnp.bfloat16).reshape(nr, -1, DH)
        ka = lax.all_gather(k, 'cp', axis=0, tiled=True)
        va = lax.all_gather(v, 'cp', axis=0, tiled=True)
        pa = lax.all_gather(pg, 'cp', axis=0, tiled=True)
        o = attend(q, ka, va, pg, pa)
        y = lax.psum_scatter(jnp.dot(o, wo, preferred_element_type=jnp.float32), 'tp', scatter_dimension=0, tiled=True)
        h1 = (x.astype(jnp.float32) + y).astype(jnp.bfloat16)
        b = lax.all_gather(rms_norm(h1, g2), 'tp', axis=0, tiled=True)
        hid = (jax.nn.silu(jnp.dot(b, w1, preferred_element_type=jnp.float32)) * jnp.dot(b, w3, preferred_element_type=jnp.float32)).astype(jnp.bfloat16)
        z = lax.psum_scatter(jnp.dot(hid, w2, preferred_element_type=jnp.float32), 'tp', scatter_dimension=0, tiled=True)
        return (h1.astype(jnp.float32) + z).astype(jnp.bfloat16)

    return jax.shard_map(local, mesh=mesh, in_specs=(tok, P(('dp', 'cp', 'tp')), P(None), P(None), col, col, col, row, col, col, row), out_specs=tok, check_vma=False)
```

profile of v0, /device:TPU:97, one launch (start us, length us, event | category | flops | bytes accessed | tf_op | source)
XLA Modules:
  0.0 1337.3 jit_solution(1085201976903756411)
XLA Ops:
  13.9 10.5 all-gather
  27.4 88.9 %all-gather.6.cloned.1.call-done = bf16[1024,5120]{1,0:T(8,128)(2,1)} async-done(((bf16[256,5120]{1,0:T(8,128)(2,1)}), bf16[1024,5120]{1,0:T(8,128)(2,1)}) %all-gather.6.cloned.1.call-update) | async-done | bytes 10485776 | tf_op jit(solution)/shard_map/all_gather | solution.py:58
  116.3 5.6 fusion.39
  125.5 7.6 convolution_convert_fusion
  134.3 20.5 %all_gather.19 = s32[8192]{0:T(1024)S(1)} all-gather(s32[1024]{0:T(1024)S(1)} %bitcast.77), channel_id=1, replica_groups=mesh['dp'=1,'tp'=4,'cp'=8] {'cp'}, dimensions={0}, use_global_device_ids=true | all-gather | bytes 36864 | tf_op jit(solution)/shard_map/all_gather | solution.py:66
  154.9 17.3 %fusion.38 = f32[1024,1280]{0,1:T(8,128)S(1)} fusion(bf16[1024,5120]{1,0:T(8,128)(2,1)} %all-gather.6.cloned.1.call-done, bf16[5120,1280]{1,0:T(8,128)(2,1)} %param.17), kind=kOutput, calls=%fused_computation.54 | convolution fusion | flops 13421772800 | bytes 28835840 | tf_op jit(solution)/shard_map/dot_general | solution.py:61
  182.4 5.0 pad_maximum_fusion
  187.5 7.3 copy.29
  194.7 492.1 %while.10 = (s32[]{:T(128)}, bf16[16,64,2,5,128]{4,1,3,2,0:T(8,128)(2,1)}, s32[8192]{0:T(1024)S(1)}, s32[16,64]{1,0:T(8,128)S(1)}, bf16[16,64,2,5,128]{4,1,3,2,0...) while((s32[]{:T(128)}, ...), condition=%wide.region_4.5_spmd, body=%wide.region_1.4_spmd.sunk | while | flops 2726912000 | bytes 93690712 | solution.py:49
  195.1 4.8 fusion.67
  200.3 13.8 %fusion.69 = (f32[2,5,64]{2,1,0:T(8,128)S(1)}, f32[2,5,64,8192]{3,2,1,0:T(8,128)}) fusion(f32[2,64,5,8192]{3,1,2,0:T(8,128)S(1)} %fusion.67, pred[64,8192]{1,0:T(8,128)(4,1)S(1)} %broadcast_compare_fusion.2), kind=kOutput, calls=%fused_computation.52.clone.1 | output fusion | flops 31465472 | bytes 42469888 | tf_op jit(solution)/shard_map/while/body/eval_jaxpr/sub | solution.py:44
  214.1 11.7 fusion.70
  225.9 4.8 fusion.67
  231.0 13.8 %fusion.69 = (f32[2,5,64]{2,1,0:T(8,128)S(1)}, f32[2,5,64,8192]{3,2,1,0:T(8,128)}) fusion(f32[2,64,5,8192]{3,1,2,0:T(8,128)S(1)} %fusion.67, pred[64,8192]{1,0:T(8,128)(4,1)S(1)} %broadcast_compare_fusion.2), kind=kOutput, calls=%fused_computation.52.clone.1 | output fusion | flops 31465472 | bytes 42469888 | tf_op jit(solution)/shard_map/while/body/eval_jaxpr/sub | solution.py:44
  244.9 11.7 fusion.70
  256.6 4.8 fusion.67
  261.8 13.8 %fusion.69 = (f32[2,5,64]{2,1,0:T(8,128)S(1)}, f32[2,5,64,8192]{3,2,1,0:T(8,128)}) fusion(f32[2,64,5,8192]{3,1,2,0:T(8,128)S(1)} %fusion.67, pred[64,8192]{1,0:T(8,128)(4,1)S(1)} %broadcast_compare_fusion.2), kind=kOutput, calls=%fused_computation.52.clone.1 | output fusion | flops 31465472 | bytes 42469888 | tf_op jit(solution)/shard_map/while/body/eval_jaxpr/sub | solution.py:44
  275.6 11.7 fusion.70
  287.3 4.8 fusion.67
  292.5 13.8 %fusion.69 = (f32[2,5,64]{2,1,0:T(8,128)S(1)}, f32[2,5,64,8192]{3,2,1,0:T(8,128)}) fusion(f32[2,64,5,8192]{3,1,2,0:T(8,128)S(1)} %fusion.67, pred[64,8192]{1,0:T(8,128)(4,1)S(1)} %broadcast_compare_fusion.2), kind=kOutput, calls=%fused_computation.52.clone.1 | output fusion | flops 31465472 | bytes 42469888 | tf_op jit(solution)/shard_map/while/body/eval_jaxpr/sub | solution.py:44
  306.3 11.7 fusion.70
  318.1 4.8 fusion.67
  323.2 13.8 %fusion.69 = (f32[2,5,64]{2,1,0:T(8,128)S(1)}, f32[2,5,64,8192]{3,2,1,0:T(8,128)}) fusion(f32[2,64,5,8192]{3,1,2,0:T(8,128)S(1)} %fusion.67, pred[64,8192]{1,0:T(8,128)(4,1)S(1)} %broadcast_compare_fusion.2), kind=kOutput, calls=%fused_computation.52.clone.1 | output fusion | flops 31465472 | bytes 42469888 | tf_op jit(solution)/shard_map/while/body/eval_jaxpr/sub | solution.py:44
  337.1 11.7 fusion.70
  348.8 4.8 fusion.67
  353.9 13.8 %fusion.69 = (f32[2,5,64]{2,1,0:T(8,128)S(1)}, f32[2,5,64,8192]{3,2,1,0:T(8,128)}) fusion(f32[2,64,5,8192]{3,1,2,0:T(8,128)S(1)} %fusion.67, pred[64,8192]{1,0:T(8,128)(4,1)S(1)} %broadcast_compare_fusion.2), kind=kOutput, calls=%fused_computation.52.clone.1 | output fusion | flops 31465472 | bytes 42469888 | tf_op jit(solution)/shard_map/while/body/eval_jaxpr/sub | solution.py:44
  367.8 11.7 fusion.70
  384.7 13.8 %fusion.69 = (f32[2,5,64]{2,1,0:T(8,128)S(1)}, f32[2,5,64,8192]{3,2,1,0:T(8,128)}) fusion(f32[2,64,5,8192]{3,1,2,0:T(8,128)S(1)} %fusion.67, pred[64,8192]{1,0:T(8,128)(4,1)S(1)} %broadcast_compare_fusion.2), kind=kOutput, calls=%fused_computation.52.clone.1 | output fusion | flops 31465472 | bytes 42469888 | tf_op jit(solution)/shard_map/while/body/eval_jaxpr/sub | solution.py:44
  398.5 11.7 fusion.70
  415.4 13.8 %fusion.69 = (f32[2,5,64]{2,1,0:T(8,128)S(1)}, f32[2,5,64,8192]{3,2,1,0:T(8,128)}) fusion(f32[2,64,5,8192]{3,1,2,0:T(8,128)S(1)} %fusion.67, pred[64,8192]{1,0:T(8,128)(4,1)S(1)} %broadcast_compare_fusion.2), kind=kOutput, calls=%fused_computation.52.clone.1 | output fusion | flops 31465472 | bytes 42469888 | tf_op jit(solution)/shard_map/while/body/eval_jaxpr/sub | solution.py:44
  429.2 11.7 fusion.70
  446.1 13.8 %fusion.69 = (f32[2,5,64]{2,1,0:T(8,128)S(1)}, f32[2,5,64,8192]{3,2,1,0:T(8,128)}) fusion(f32[2,64,5,8192]{3,1,2,0:T(8,128)S(1)} %fusion.67, pred[64,8192]{1,0:T(8,128)(4,1)S(1)} %broadcast_compare_fusion.2), kind=kOutput, calls=%fused_computation.52.clone.1 | output fusion | flops 31465472 | bytes 42469888 | tf_op jit(solution)/shard_map/while/body/eval_jaxpr/sub | solution.py:44
  460.0 11.7 fusion.70
  476.9 13.8 %fusion.69 = (f32[2,5,64]{2,1,0:T(8,128)S(1)}, f32[2,5,64,8192]{3,2,1,0:T(8,128)}) fusion(f32[2,64,5,8192]{3,1,2,0:T(8,128)S(1)} %fusion.67, pred[64,8192]{1,0:T(8,128)(4,1)S(1)} %broadcast_compare_fusion.2), kind=kOutput, calls=%fused_computation.52.clone.1 | output fusion | flops 31465472 | bytes 42469888 | tf_op jit(solution)/shard_map/while/body/eval_jaxpr/sub | solution.py:44
  490.7 11.7 fusion.70
  502.4 4.8 fusion.67
  507.6 13.8 %fusion.69 = (f32[2,5,64]{2,1,0:T(8,128)S(1)}, f32[2,5,64,8192]{3,2,1,0:T(8,128)}) fusion(f32[2,64,5,8192]{3,1,2,0:T(8,128)S(1)} %fusion.67, pred[64,8192]{1,0:T(8,128)(4,1)S(1)} %broadcast_compare_fusion.2), kind=kOutput, calls=%fused_computation.52.clone.1 | output fusion | flops 31465472 | bytes 42469888 | tf_op jit(solution)/shard_map/while/body/eval_jaxpr/sub | solution.py:44
  521.4 11.7 fusion.70
  533.2 4.8 fusion.67
  538.3 13.8 %fusion.69 = (f32[2,5,64]{2,1,0:T(8,128)S(1)}, f32[2,5,64,8192]{3,2,1,0:T(8,128)}) fusion(f32[2,64,5,8192]{3,1,2,0:T(8,128)S(1)} %fusion.67, pred[64,8192]{1,0:T(8,128)(4,1)S(1)} %broadcast_compare_fusion.2), kind=kOutput, calls=%fused_computation.52.clone.1 | output fusion | flops 31465472 | bytes 42469888 | tf_op jit(solution)/shard_map/while/body/eval_jaxpr/sub | solution.py:44
  552.2 11.7 fusion.70
  563.9 4.8 fusion.67
  569.0 13.8 %fusion.69 = (f32[2,5,64]{2,1,0:T(8,128)S(1)}, f32[2,5,64,8192]{3,2,1,0:T(8,128)}) fusion(f32[2,64,5,8192]{3,1,2,0:T(8,128)S(1)} %fusion.67, pred[64,8192]{1,0:T(8,128)(4,1)S(1)} %broadcast_compare_fusion.2), kind=kOutput, calls=%fused_computation.52.clone.1 | output fusion | flops 31465472 | bytes 42469888 | tf_op jit(solution)/shard_map/while/body/eval_jaxpr/sub | solution.py:44
  582.9 11.7 fusion.70
  594.6 4.8 fusion.67
  599.8 13.8 %fusion.69 = (f32[2,5,64]{2,1,0:T(8,128)S(1)}, f32[2,5,64,8192]{3,2,1,0:T(8,128)}) fusion(f32[2,64,5,8192]{3,1,2,0:T(8,128)S(1)} %fusion.67, pred[64,8192]{1,0:T(8,128)(4,1)S(1)} %broadcast_compare_fusion.2), kind=kOutput, calls=%fused_computation.52.clone.1 | output fusion | flops 31465472 | bytes 42469888 | tf_op jit(solution)/shard_map/while/body/eval_jaxpr/sub | solution.py:44
  613.6 11.7 fusion.70
  625.3 4.8 fusion.67
  630.5 13.8 %fusion.69 = (f32[2,5,64]{2,1,0:T(8,128)S(1)}, f32[2,5,64,8192]{3,2,1,0:T(8,128)}) fusion(f32[2,64,5,8192]{3,1,2,0:T(8,128)S(1)} %fusion.67, pred[64,8192]{1,0:T(8,128)(4,1)S(1)} %broadcast_compare_fusion.2), kind=kOutput, calls=%fused_computation.52.clone.1 | output fusion | flops 31465472 | bytes 42469888 | tf_op jit(solution)/shard_map/while/body/eval_jaxpr/sub | solution.py:44
  644.3 11.7 fusion.70
  656.1 4.8 fusion.67
  661.2 13.8 %fusion.69 = (f32[2,5,64]{2,1,0:T(8,128)S(1)}, f32[2,5,64,8192]{3,2,1,0:T(8,128)}) fusion(f32[2,64,5,8192]{3,1,2,0:T(8,128)S(1)} %fusion.67, pred[64,8192]{1,0:T(8,128)(4,1)S(1)} %broadcast_compare_fusion.2), kind=kOutput, calls=%fused_computation.52.clone.1 | output fusion | flops 31465472 | bytes 42469888 | tf_op jit(solution)/shard_map/while/body/eval_jaxpr/sub | solution.py:44
  675.1 11.7 fusion.70
  686.8 5.9 copy.30
  692.7 6.0 reshape.130
  698.7 20.6 %fusion.40 = f32[1024,5120]{1,0:T(8,128)} fusion(bf16[1024,1280]{1,0:T(8,128)(2,1)S(1)} %reshape.130, bf16[1280,5120]{1,0:T(8,128)(2,1)} %param.20), kind=kOutput, calls=%fused_computation.56 | convolution fusion | flops 13421772800 | bytes 36700160 | tf_op jit(solution)/shard_map/dot_general | solution.py:68
  720.0 181.3 %reduce-scatter.3.cloned.1.call-done = f32[256,5120]{1,0:T(8,128)} async-done(((f32[1024,5120]{1,0:T(8,128)}), f32[256,5120]{1,0:T(8,128)}) %reduce-scatter.3.cloned.1.call-update) | async-done | bytes 5242896 | tf_op jit(solution)/shard_map/reduce_scatter | solution.py:68
  901.3 5.0 fusion.31
  910.5 98.4 %all-gather.12.cloned.1.call-done = bf16[1024,5120]{1,0:T(8,128)(2,1)} async-done(((bf16[256,5120]{1,0:T(8,128)(2,1)}), bf16[1024,5120]{1,0:T(8,128)(2,1)}) %all-gather.12.cloned.1.call-update) | async-done | bytes 10485776 | tf_op jit(solution)/shard_map/all_gather | solution.py:70
  1008.9 47.1 %fusion.41 = f32[1024,3456]{1,0:T(8,128)} fusion(bf16[1024,5120]{1,0:T(8,128)(2,1)} %all-gather.12.cloned.1.call-done, bf16[5120,3456]{1,0:T(8,128)(2,1)} %param.21), kind=kOutput, calls=%fused_computation.57 | convolution fusion | flops 36238786560 | bytes 60030976 | tf_op jit(solution)/shard_map/dot_general | solution.py:71
  1056.0 44.1 %multiply_convert_fusion = bf16[1024,3456]{1,0:T(8,128)(2,1)S(1)} fusion(f32[1024,3456]{1,0:T(8,128)} %fusion.41, bf16[1024,5120]{1,0:T(8,128)(2,1)S(1)} %copy-done.5, bf16[5120,3456]{1,0:T(8,128)(2,1)} %param.22), kind=kOutput, calls=%fused_computation.25 | convolution fusion | flops 36260020224 | bytes 67108864 | tf_op jit(solution)/shard_map/dot_general | solution.py:71
  1100.1 44.2 %fusion.42 = f32[1024,5120]{1,0:T(8,128)} fusion(bf16[1024,3456]{1,0:T(8,128)(2,1)S(1)} %multiply_convert_fusion, bf16[3456,5120]{1,0:T(8,128)(2,1)} %param.23), kind=kOutput, calls=%fused_computation.58 | convolution fusion | flops 36238786560 | bytes 63438848 | tf_op jit(solution)/shard_map/dot_general | solution.py:72
  1144.3 180.5 %reduce-scatter.5.cloned.1.call-done = f32[256,5120]{1,0:T(8,128)} async-done(((f32[1024,5120]{1,0:T(8,128)}), f32[256,5120]{1,0:T(8,128)}) %reduce-scatter.5.cloned.1.call-update) | async-done | bytes 5242896 | tf_op jit(solution)/shard_map/reduce_scatter | solution.py:72
  1324.8 5.5 fusion.34
  (86 shorter events, 54.9 us)
Async XLA Ops:
  6.5 109.8 %copy-start = (bf16[5120,256]{1,0:T(8,128)(2,1)S(1)}, bf16[5120,256]{1,0:T(8,128)(2,1)}, u32[]{:S(2)}) copy-start(bf16[5120,256]{1,0:T(8,128)(2,1)} %param.18) | copy-start | bytes 7864324
  6.6 109.8 %all-gather.6.cloned.1.call-start = ((), (), s32[]{:S(2)}) async-start(), calls=%async_computation.2 | async-start | bytes 13107200 | tf_op jit(solution)/shard_map/all_gather | solution.py:58
  7.4 6.5 copy-start.4
  13.8 180.9 %all-gather.8.cloned.1.call-start = ((), (), s32[]{:S(2)}) async-start(), calls=%async_computation.3 | async-start | bytes 4718592 | tf_op jit(solution)/shard_map/all_gather | solution.py:64
  125.4 69.4 %all-gather.10.cloned.1.call-start = ((), (), s32[]{:S(2)}) async-start(), calls=%async_computation.4 | async-start | bytes 4718592 | tf_op jit(solution)/shard_map/all_gather | solution.py:65
  134.2 767.1 %reduce-scatter.3.cloned.1.call-start = ((), (), s32[]{:S(2)}) async-start(), calls=%async_computation.5 | async-start | bytes 26214400 | tf_op jit(solution)/shard_map/reduce_scatter | solution.py:68
  719.3 0.7 copy-start.3
  719.3 182.0 %copy-start.2 = (bf16[256,5120]{1,0:T(8,128)(2,1)S(1)}, bf16[256,5120]{1,0:T(8,128)(2,1)}, u32[]{:S(2)}) copy-start(bf16[256,5120]{1,0:T(8,128)(2,1)} %param.13) | copy-start | bytes 7864324
  719.4 289.5 %all-gather.12.cloned.1.call-start = ((), (), s32[]{:S(2)}) async-start(), calls=%async_computation.6 | async-start | bytes 13107200 | tf_op jit(solution)/shard_map/all_gather | solution.py:70
  910.4 414.4 %reduce-scatter.5.cloned.1.call-start = ((), (), s32[]{:S(2)}) async-start(), calls=%async_computation.7 | async-start | bytes 26214400 | tf_op jit(solution)/shard_map/reduce_scatter | solution.py:72
  1008.9 47.1 %copy-start.5 = (bf16[1024,5120]{1,0:T(8,128)(2,1)S(1)}, bf16[1024,5120]{1,0:T(8,128)(2,1)}, u32[]{:S(2)}) copy-start(bf16[1024,5120]{1,0:T(8,128)(2,1)} %all-gather.12.cloned.1.call-done) | copy-start | bytes 31457284
  1144.3 186.0 %copy-start.1 = (bf16[5120,256]{1,0:T(8,128)(2,1)S(1)}, bf16[5120,256]{1,0:T(8,128)(2,1)}, u32[]{:S(2)}) copy-start(bf16[5120,256]{1,0:T(8,128)(2,1)} %param.18) | copy-start | bytes 7864324
Sparse Core Ops, SparseCore 0:
  14.0 102.3 all-gather.5
  125.5 31.4 all-gather.7
  158.6 29.1 all-gather.9
  719.5 181.7 reduce-scatter.2
  910.5 98.3 all-gather.11
  1144.4 180.3 reduce-scatter.4
where the time goes:
time: 1340 us
  waiting for transfers between devices  549 us (41%)
  matrix products  451 us (34%)
  other arithmetic  260 us (19%)
  local copies, waits for them, and re-layouts  31.6 us (2%)
  blocking collectives  31 us (2%)
  between operations  13.8 us (1%)
    sub x16, other arithmetic, blk(): e = jnp.exp(s - jnp.max(s, axis=-1, keepdims=True))  221 us
    dot_general x16, matrix products, blk(): o = jnp.einsum('kgqs,skd->qkgd', w, v, preferred_element_type=jnp.float32)  188 us
    reduce_scatter x1, waiting for transfers between devices, local(): lax.psum_scatter(jnp.dot(o, wo, preferred_element_type=jnp.float32), 'tp'...  181 us
    reduce_scatter x1, waiting for transfers between devices, local(): lax.psum_scatter(jnp.dot(hid, w2, preferred_element_type=jnp.float32), 't...  180 us
    all_gather x1, waiting for transfers between devices, local(): b = lax.all_gather(rms_norm(h1, g2), 'tp', axis=0, tiled=True)  98.4 us
    all_gather x1, waiting for transfers between devices, local(): a = lax.all_gather(rms_norm(x, g1), 'tp', axis=0, tiled=True)  88.9 us
    dot_general x16, matrix products, blk(): jnp.einsum('qkgd,skd->kgqs', qq, k, preferred_element_type=jnp.float32)  76.4 us
    dot_general x1, matrix products, local(): jnp.dot(b, w1, preferred_element_type=jnp.float32)  47.1 us
  transfers between devices with their start and end apart: 6, of which 4 were waited for; matrix products, arithmetic and copies ran while one was open for 4% of the time, Pallas kernels for 0%

commit v1 on v0

v1 whole, which is shorter than its diff:
```python
import functools
import math

import jax
import jax.numpy as jnp
from jax import lax
from jax.experimental import pallas as pl
from jax.experimental.pallas import tpu as pltpu
from jax.sharding import PartitionSpec as P

DH = 128
EPS = 1e-5
THETA = 500000.0
NEG = -1e30


def rms_norm(v, g):
    vf = v.astype(jnp.float32)
    inv = lax.rsqrt(jnp.mean(vf * vf, axis=-1, keepdims=True) + EPS)
    return (vf * inv * g.astype(jnp.float32)).astype(jnp.bfloat16)


def tables(p):
    freq = 1.0 / (THETA ** (jnp.arange(0, DH, 2, dtype=jnp.float32) / DH))
    ang = p.astype(jnp.float32)[:, None] * freq
    c = jnp.cos(ang)
    s = jnp.sin(ang)
    return jnp.concatenate([c, c], axis=1), jnp.concatenate([-s, s], axis=1)


def dot32(a, b):
    return jnp.dot(a, b, preferred_element_type=jnp.float32)


def kv_kernel(u_ref, c_ref, s_ref, o_ref):
    kw = u_ref.shape[1] // 2
    c = c_ref[...]
    s = s_ref[...]
    for h in range(kw // DH):
        u = u_ref[:, h * DH:(h + 1) * DH]
        o_ref[:, h * DH:(h + 1) * DH] = (u * c + pltpu.roll(u, DH // 2, 1) * s).astype(jnp.bfloat16)
    o_ref[:, kw:] = u_ref[:, kw:].astype(jnp.bfloat16)


def kv_finish(u, c, s):
    return pl.pallas_call(
        kv_kernel,
        out_shape=jax.ShapeDtypeStruct(u.shape, jnp.bfloat16),
        cost_estimate=pl.CostEstimate(flops=2 * 10**9, bytes_accessed=6 * u.size, transcendentals=0),
        name="kv_finish",
    )(u, c, s)


LOW = (0, -1, 2, 1)
HIGH = (0, 1, 2, -1)


def attn_kernel(ntp, ncp, bat, info_ref, q_ref, c_ref, s_ref, *rest):
    kvs = rest[:8]
    o_ref, kv, qs, acc, ms, ls, sem = rest[8:]
    piece = q_ref.shape[0] // 2
    heads = q_ref.shape[1] // DH
    kvh = kv.shape[1] // (2 * DH)
    grp = heads // kvh
    mrow = grp * piece
    blk = ntp * piece
    npc = 2 * ntp * ncp
    cc = info_ref[0]
    jj = info_ref[1]

    copies = []
    for b in range(4):
        for side in range(2):
            src = kvs[2 * b + side]
            core = lax.rem(cc, 2)
            c0 = cc if side == 0 else cc + 1 - 2 * core
            for e, d in enumerate((0, ncp - 2, 2, 4)):
                ce = lax.rem(c0 + d, ncp)
                for half in range(2):
                    off = (LOW, HIGH)[half][b]
                    k = ce * ntp + lax.rem(jj + off + ntp, ntp)
                    p = k if half == 0 else npc - 1 - k
                    copies.append(pltpu.make_async_copy(
                        src.at[pl.ds((2 * e + half) * piece, piece), :],
                        kv.at[pl.ds(pl.multiple_of(p * piece, piece), piece), :],
                        sem))
    for c in copies:
        c.start()

    for half in range(2):
        r0 = half * piece
        c = c_ref[r0:r0 + piece, :]
        s = s_ref[r0:r0 + piece, :]
        for h in range(heads):
            u = q_ref[r0:r0 + piece, h * DH:(h + 1) * DH]
            qs[half, h // grp, (h % grp) * piece:(h % grp + 1) * piece, :] = (
                u * c + pltpu.roll(u, DH // 2, 1) * s).astype(jnp.bfloat16)

    for c in copies:
        c.wait()

    scale = math.log2(math.e) / math.sqrt(DH)
    for half in range(2):
        ms[...] = jnp.full_like(ms, NEG)
        ls[...] = jnp.zeros_like(ls)
        acc[...] = jnp.zeros_like(acc)
        k = cc * ntp + lax.rem(jj + (LOW, HIGH)[half][bat] + ntp, ntp)
        pq = k if half == 0 else npc - 1 - k
        nfull = cc if half == 0 else 2 * ncp - 1 - cc

        def step(i, masked, half=half, pq=pq):
            k0 = pl.multiple_of(i * blk, blk)
            for g in range(kvh):
                kk = kv[pl.ds(k0, blk), g * DH:(g + 1) * DH]
                vv = kv[pl.ds(k0, blk), (kvh + g) * DH:(kvh + g + 1) * DH]
                s = lax.dot_general(qs[half, g], kk, (((1,), (1,)), ((), ())),
                                    preferred_element_type=jnp.float32)
                if masked:
                    row = lax.broadcasted_iota(jnp.int32, (mrow, blk), 0)
                    row = lax.rem(row, piece) + pq * piece
                    col = lax.broadcasted_iota(jnp.int32, (mrow, blk), 1) + k0
                    s = jnp.where(col <= row, s, NEG)
                m_old = ms[g]
                m_new = jnp.maximum(m_old, jnp.max(s, axis=1, keepdims=True))
                alpha = jnp.exp2((m_old - m_new) * scale)
                ms[g] = m_new
                ps = []
                lsum = ls[g] * alpha
                for t in range(blk // DH):
                    pt = jnp.exp2((s[:, t * DH:(t + 1) * DH] - m_new) * scale)
                    lsum = lsum + pt
                    ps.append(pt.astype(jnp.bfloat16))
                ls[g] = lsum
                pv = jnp.dot(jnp.concatenate(ps, axis=1), vv, preferred_element_type=jnp.float32)
                acc[g] = acc[g] * alpha + pv

        lax.fori_loop(0, nfull, lambda i, z: (step(i, False), z)[1], 0)
        step(nfull, True)
        for g in range(kvh):
            o = acc[g] / jnp.sum(ls[g], axis=1, keepdims=True)
            for h in range(grp):
                hh = g * grp + h
                o_ref[half * piece:(half + 1) * piece, hh * DH:(hh + 1) * DH] = (
                    o[h * piece:(h + 1) * piece, :].astype(jnp.bfloat16))


def attend(bat, ntp, ncp, info, q, c, s, kvs):
    rows, width = q.shape
    piece = rows // 2
    kvw = kvs[0].shape[1]
    kvh = kvw // (2 * DH)
    mrow = (width // DH // kvh) * piece
    total = 2 * ntp * ncp * piece
    vm = pl.BlockSpec(memory_space=pltpu.VMEM)
    return pl.pallas_call(
        functools.partial(attn_kernel, ntp, ncp, bat),
        out_shape=jax.ShapeDtypeStruct((rows, width), jnp.bfloat16),
        in_specs=[pl.BlockSpec(memory_space=pltpu.SMEM), vm, vm, vm] + [pl.BlockSpec(memory_space=pltpu.HBM)] * 8,
        out_specs=vm,
        scratch_shapes=[
            pltpu.VMEM((total, kvw), jnp.bfloat16),
            pltpu.VMEM((2, kvh, mrow, DH), jnp.bfloat16),
            pltpu.VMEM((kvh, mrow, DH), jnp.float32),
            pltpu.VMEM((kvh, mrow, DH), jnp.float32),
            pltpu.VMEM((kvh, mrow, DH), jnp.float32),
            pltpu.SemaphoreType.DMA,
        ],
        compiler_params=pltpu.CompilerParams(vmem_limit_bytes=40 * 2**20),
        cost_estimate=pl.CostEstimate(
            flops=2 * 10**10, bytes_accessed=2 * total * kvw + 6 * q.size, transcendentals=rows * width // DH * total // 2),
    )(info, q, c, s, *kvs)


def solution(mesh):
    tok = P(('dp', 'cp', 'tp'), None)
    col = P(None, 'tp')
    row = P('tp', None)
    ntp = mesh.shape['tp']
    ncp = mesh.shape['cp']
    assert ntp == 4 and ncp == 8

    def tshift(v, d):
        return lax.ppermute(v, 'tp', [(i, (i + d) % ntp) for i in range(ntp)])

    def cshift(v, d):
        return lax.ppermute(v, 'cp', [(i, (i + d) % ncp) for i in range(ncp)])

    def cswap(v):
        return lax.ppermute(v, 'cp', [(i, i ^ 1) for i in range(ncp)])

    def cat(u, v):
        return jnp.concatenate([u, v], axis=0)

    def gather(lo, hi):
        p_lo = tshift(lo, 1)
        m_hi = tshift(hi, -1)
        p_hi = tshift(hi, 1)
        m_lo = tshift(lo, -1)
        f_lo = tshift(p_lo, 1)
        f_hi = tshift(m_hi, -1)
        return (p_lo, m_hi), (f_lo, f_hi), (m_lo, p_hi)

    def layer(x, pos, g1, g2, wq, wk, wv, wo, w1, w3, w2):
        n = x.shape[0]
        h = n // 2
        pos_p = tshift(pos, 1)
        pos_m = tshift(pos, -1)
        pos_2 = tshift(pos, 2)
        info = jnp.stack([lax.axis_index('cp'), lax.axis_index('tp')]).astype(jnp.int32)

        lo = rms_norm(x[:h], g1)
        hi = rms_norm(x[h:], g1)
        parts = [(lo, hi)] + list(gather(lo, hi))
        ptab = [pos, cat(pos_p[:h], pos_m[h:]), pos_2, cat(pos_m[:h], pos_p[h:])]
        tabs = [tables(p) for p in ptab]
        wkv = jnp.concatenate([wk, wv], axis=1)

        qs, kvs = [], []
        for b in range(4):
            a = cat(*parts[b])
            kvu = dot32(a, wkv)
            kv = kv_finish(kvu, *tabs[b])
            others = [cshift(kv, 2), cshift(kv, -2), cshift(kv, 4)]
            stack = jnp.concatenate([kv] + others, axis=0)
            kvs += [stack, cswap(stack)]
            qs.append(dot32(a, wq))

        def attn(b):
            return attend(b, ntp, ncp, info, qs[b], *tabs[b], kvs)

        def scatter(part):
            y = part(1).astype(jnp.bfloat16)
            r1_lo = tshift(y[:h], -1)
            r1_hi = tshift(y[h:], 1)
            y = part(2).astype(jnp.bfloat16)
            s_lo = tshift(y[:h], 1)
            s_hi = tshift(y[h:], -1)
            y = lax.optimization_barrier(part(3))
            y_lo = (y[:h] + s_lo.astype(jnp.float32)).astype(jnp.bfloat16)
            y_hi = (y[h:] + s_hi.astype(jnp.float32)).astype(jnp.bfloat16)
            r3_lo = tshift(y_lo, 1)
            r3_hi = tshift(y_hi, -1)
            y = part(0)
            return y, (r1_lo, r1_hi), (r3_lo, r3_hi)

        def total(base, y, r1, r3, i):
            t = base.astype(jnp.float32) + y + r1[i].astype(jnp.float32) + r3[i].astype(jnp.float32)
            return t.astype(jnp.bfloat16)

        y, r1, r3 = scatter(lambda b: dot32(attn(b), wo))
        h_lo = total(x[:h], y[:h], r1, r3, 0)
        h_hi = total(x[h:], y[h:], r1, r3, 1)

        lo = rms_norm(h_lo, g2)
        hi = rms_norm(h_hi, g2)
        parts2 = [(lo, hi)] + list(gather(lo, hi))
        hid = []
        for b in range(4):
            a = cat(*parts2[b])
            hid.append((jax.nn.silu(dot32(a, w1)) * dot32(a, w3)).astype(jnp.bfloat16))
        y, r1, r3 = scatter(lambda b: dot32(hid[b], w2))
        return cat(total(h_lo, y[:h], r1, r3, 0), total(h_hi, y[h:], r1, r3, 1))

    return jax.shard_map(layer, mesh=mesh, in_specs=(tok, P(('dp', 'cp', 'tp')), P(None), P(None), col, col, col, row, col, col, row),
                         out_specs=tok, check_vma=False)
```

time: 1340 us -> 657 us (0.49)
  the two profiles are of different devices: /device:TPU:97 before, /device:TPU:102 now
where the time goes in v1:
time: 657 us; the launch traced here: 648 us
  matrix products  293 us (45%)
  Pallas kernels  146 us (22%)
  waiting for transfers between devices  92.6 us (14%)
  starting transfers between devices  59.1 us (9%)
  other arithmetic  31.5 us (5%)
  local copies, waits for them, and re-layouts  24.1 us (4%)
    dot_general x21, matrix products, dot32(): return jnp.dot(a, b, preferred_element_type=jnp.float32)  293 us
    pallas_call x4, Pallas kernels, attend(): pl.pallas_call(functools.partial(attn_kernel, ntp, ncp, bat), out_shape=j...  139 us
    ppermute x27, waiting for transfers between devices, tshift(): return lax.ppermute(v, 'tp', [(i, (i + d) % ntp) for i in range(ntp)])  78.3 us
    ppermute x27, starting transfers between devices, tshift(): return lax.ppermute(v, 'tp', [(i, (i + d) % ntp) for i in range(ntp)])  42.8 us
    ppermute x12, starting transfers between devices, cshift(): return lax.ppermute(v, 'cp', [(i, (i + d) % ncp) for i in range(ncp)])  15.4 us
    unnamed x77, local copies, waits for them, and re-layouts  14.4 us
    ppermute x12, waiting for transfers between devices, cshift(): return lax.ppermute(v, 'cp', [(i, (i + d) % ncp) for i in range(ncp)])  14.3 us
  transfers between devices with their start and end apart: 43, of which 9 were waited for; matrix products, arithmetic and copies ran while one was open for 49% of the time, Pallas kernels for 17%

profile of v1, /device:TPU:102, one launch (start us, length us, event | category | flops | bytes accessed | tf_op | source)
XLA Modules:
  0.0 648.3 jit_solution(17316901973569334235)
XLA Ops:
  0.0 2.1 collective-permute-start.6
  2.1 2.6 collective-permute-start.7
  6.3 2.3 fusion.1
  9.4 2.4 fusion.9
  15.7 2.7 copy-done.18
  18.4 4.8 fusion.35.u_ref
  23.2 6.5 %fusion.36.q_ref = f32[256,1280]{1,0:T(8,128)} fusion(bf16[5120,1280]{1,0:T(8,128)(2,1)S(1)} %copy-done.34, bf16[128,5120]{1,0:T(8,128)(2,1)} %get-tuple-element.19, bf16[128,5120]{1,0:T(8,128)(2,1)} %get-tuple-element.20), kind=kOutput, calls=%fused_computation.63 | convolution fusion | flops 3360686080 | bytes 17039360 | tf_op jit(solution)/shard_map/dot_general | solution.py:32
  30.4 1.9 fusion.39
  33.8 2.0 kv_finish.4
  35.9 2.0 collective-permute-start.1
  43.5 1.7 collective-permute-done
  46.4 3.2 collective-permute-done.1
  49.6 2.0 collective-permute-start.5
  55.7 4.9 fusion.66.u_ref
  60.6 2.0 kv_finish.7
  62.6 2.2 collective-permute-start.22
  65.7 7.8 %collective-permute-done.4 = bf16[128,5120]{1,0:T(8,128)(2,1)} collective-permute-done((bf16[128,5120]{1,0:T(8,128)(2,1)}, bf16[128,5120]{1,0:T(8,128)(2,1)}, u32[]{:S(2)}, u32[]{:S(2)}) %collective-permute-start.4) | collective-permute-done | bytes 1310752 | tf_op jit(solution)/shard_map/ppermute | solution.py:183
  76.3 4.8 fusion.64.u_ref
  81.1 7.8 %fusion.68.q_ref = f32[256,1280]{1,0:T(8,128)} fusion(bf16[256,5120]{1,0:T(8,128)(2,1)S(1)} %constant_dynamic-update-slice_fusion.2, bf16[5120,1280]{1,0:T(8,128)(2,1)} %param.15), kind=kOutput, calls=%fused_computation.131 | convolution fusion | flops 3355443200 | bytes 17039360 | tf_op jit(solution)/shard_map/dot_general | solution.py:32
  88.9 3.2 collective-permute-start.13
  92.1 2.0 kv_finish.5
  94.1 8.1 %fusion.69.q_ref = f32[256,1280]{1,0:T(8,128)S(1)} fusion(bf16[256,5120]{1,0:T(8,128)(2,1)} %copy-done.27, bf16[5120,1280]{1,0:T(8,128)(2,1)} %param.15), kind=kOutput, calls=%fused_computation.132 | convolution fusion | flops 3355443200 | bytes 17039360 | tf_op jit(solution)/shard_map/dot_general | solution.py:32
  102.2 14.1 %collective-permute-done.12 = bf16[128,5120]{1,0:T(8,128)(2,1)} collective-permute-done((bf16[128,5120]{1,0:T(8,128)(2,1)}, bf16[128,5120]{1,0:T(8,128)(2,1)}, u32[]{:S(2)}, u32[]{:S(2)}) %collective-permute-start.12) | collective-permute-done | bytes 1310752 | tf_op jit(solution)/shard_map/ppermute | solution.py:183
  116.3 3.7 collective-permute-start.10
  123.1 5.8 fusion.65.u_ref
  128.9 1.8 collective-permute-start.9
  130.8 2.0 kv_finish.6
  136.3 5.7 collective-permute-done.9
  143.9 3.6 collective-permute-done.16
  147.7 6.8 %fusion.71.q_ref = f32[256,1280]{1,0:T(8,128)S(1)} fusion(bf16[256,5120]{1,0:T(8,128)(2,1)S(1)} %copy-done.24, bf16[5120,1280]{1,0:T(8,128)(2,1)} %param.15), kind=kOutput, calls=%fused_computation.134 | convolution fusion | flops 3355443200 | bytes 17039360 | tf_op jit(solution)/shard_map/dot_general | solution.py:32
  154.6 34.9 %shard_map.110 = bf16[256,1280]{1,0:T(8,128)(2,1)S(1)} custom-call(s32[2]{0:T(128)S(1)} %pad_add_fusion.info_ref, f32[256,1280]{1,0:T(8,128)S(1)} %copy-done.8, f32[256,128]{1,0:T(8,128)S(1)} %copy-done.7, f32[256,128]{1,0:T(8,128)S(1)} %copy-done.3, bf16[1024,512]{1,0:T(8,128)(2,1)S(1)} %pad_maximum_fusion.9.rest_0_, ...), custom_call_target="tpu_custom_call" | custom-call | flops 20000000000 | bytes 10354688 | tf_op jit(solution)/shard_map/pallas_call | solution.py:155
  189.5 8.7 %convolution_convert_fusion.1 = bf16[256,5120]{1,0:T(8,128)(2,1)S(1)} fusion(bf16[256,1280]{1,0:T(8,128)(2,1)S(1)} %shard_map.110, bf16[1280,5120]{1,0:T(8,128)(2,1)} %param.18), kind=kOutput, calls=%fused_computation.1 | convolution fusion | flops 3356753920 | bytes 16384000 | tf_op jit(solution)/shard_map/dot_general | solution.py:32
  200.6 34.7 %shard_map.112 = bf16[256,1280]{1,0:T(8,128)(2,1)S(1)} custom-call(s32[2]{0:T(128)S(1)} %pad_add_fusion.info_ref, f32[256,1280]{1,0:T(8,128)S(1)} %fusion.71.q_ref, f32[256,128]{1,0:T(8,128)S(1)} %copy-done.6, f32[256,128]{1,0:T(8,128)S(1)} %copy-done.2, bf16[1024,512]{1,0:T(8,128)(2,1)S(1)} %pad_maximum_fusion.9.rest_0_, ...), custom_call_target="tpu_custom_call" | custom-call | flops 20000000000 | bytes 10354688 | tf_op jit(solution)/shard_map/pallas_call | solution.py:155
  235.2 8.7 %convolution_convert_fusion = bf16[256,5120]{1,0:T(8,128)(2,1)S(1)} fusion(bf16[256,1280]{1,0:T(8,128)(2,1)S(1)} %shard_map.112, bf16[1280,5120]{1,0:T(8,128)(2,1)} %param.18), kind=kOutput, calls=%fused_computation | convolution fusion | flops 3356753920 | bytes 16384000 | tf_op jit(solution)/shard_map/dot_general | solution.py:32
  244.2 3.2 collective-permute-start.29
  247.5 34.5 %shard_map.111 = bf16[256,1280]{1,0:T(8,128)(2,1)S(1)} custom-call(s32[2]{0:T(128)S(1)} %pad_add_fusion.info_ref, f32[256,1280]{1,0:T(8,128)S(1)} %fusion.69.q_ref, f32[256,128]{1,0:T(8,128)S(1)} %copy-done.5, f32[256,128]{1,0:T(8,128)S(1)} %copy-done.1, bf16[1024,512]{1,0:T(8,128)(2,1)S(1)} %pad_maximum_fusion.9.rest_0_, ...), custom_call_target="tpu_custom_call" | custom-call | flops 20000000000 | bytes 10354688 | tf_op jit(solution)/shard_map/pallas_call | solution.py:155
  282.0 6.6 %fusion.70 = f32[256,5120]{1,0:T(8,128)S(1)} fusion(bf16[256,1280]{1,0:T(8,128)(2,1)S(1)} %shard_map.111, bf16[1280,5120]{1,0:T(8,128)(2,1)} %param.18), kind=kOutput, calls=%fused_computation.133 | convolution fusion | flops 3355443200 | bytes 19005440 | tf_op jit(solution)/shard_map/dot_general | solution.py:32
  289.6 3.4 collective-permute-start.30
  293.0 34.5 %shard_map.109 = bf16[256,1280]{1,0:T(8,128)(2,1)S(1)} custom-call(s32[2]{0:T(128)S(1)} %pad_add_fusion.info_ref, f32[256,1280]{1,0:T(8,128)S(1)} %copy-done.9, f32[256,128]{1,0:T(8,128)S(1)} %copy-done.4, f32[256,128]{1,0:T(8,128)S(1)} %copy-done, bf16[1024,512]{1,0:T(8,128)(2,1)S(1)} %pad_maximum_fusion.9.rest_0_, ...), custom_call_target="tpu_custom_call" | custom-call | flops 20000000000 | bytes 10354688 | tf_op jit(solution)/shard_map/pallas_call | solution.py:155
  327.6 6.8 %fusion.67 = f32[256,5120]{1,0:T(8,128)S(1)} fusion(bf16[256,1280]{1,0:T(8,128)(2,1)S(1)} %shard_map.109, bf16[1280,5120]{1,0:T(8,128)(2,1)} %param.18), kind=kOutput, calls=%fused_computation.130 | convolution fusion | flops 3355443200 | bytes 19005440 | tf_op jit(solution)/shard_map/dot_general | solution.py:32
  334.4 1.8 fusion.13
  336.3 2.4 fusion.15
  338.7 3.2 collective-permute-start.34
  342.0 2.5 collective-permute-start.35
  344.4 18.1 %fusion.33 = f32[256,3456]{1,0:T(8,128)} fusion(bf16[5120,3456]{1,0:T(8,128)(2,1)} %param.19, bf16[128,5120]{1,0:T(8,128)(2,1)} %get-tuple-element.30, bf16[128,5120]{1,0:T(8,128)(2,1)} %get-tuple-element.29), kind=kOutput, calls=%fused_computation.60 | convolution fusion | flops 9064939520 | bytes 41549824 | tf_op jit(solution)/shard_map/dot_general | solution.py:32
  362.5 18.7 %fusion.clone.4 = bf16[256,3456]{1,0:T(8,128)(2,1)} fusion(bf16[5120,3456]{1,0:T(8,128)(2,1)} %param.20, f32[256,3456]{1,0:T(8,128)} %fusion.33, bf16[128,5120]{1,0:T(8,128)(2,1)} %get-tuple-element.30, bf16[128,5120]{1,0:T(8,128)(2,1)} %get-tuple-element.29), kind=kOutput, calls=%fused_computation.5.clone.clone.clone.1 | convolution fusion | flops 9070247936 | bytes 43319296 | tf_op jit(solution)/shard_map/dot_general | solution.py:32
  381.3 15.6 %collective-permute-done.32 = bf16[128,5120]{1,0:T(8,128)(2,1)S(1)} collective-permute-done((bf16[128,5120]{1,0:T(8,128)(2,1)}, bf16[128,5120]{1,0:T(8,128)(2,1)S(1)}, u32[]{:S(2)}, u32[]{:S(2)}) %collective-permute-start.32) | collective-permute-done | bytes 1310752 | tf_op jit(solution)/shard_map/ppermute | solution.py:183
  399.5 17.8 %fusion.72 = f32[256,3456]{1,0:T(8,128)} fusion(bf16[256,5120]{1,0:T(8,128)(2,1)S(1)} %constant_dynamic-update-slice_fusion.8, bf16[5120,3456]{1,0:T(8,128)(2,1)} %param.19), kind=kOutput, calls=%fused_computation.135 | convolution fusion | flops 9059696640 | bytes 41549824 | tf_op jit(solution)/shard_map/dot_general | solution.py:32
  417.3 34.5 %convolution_convert_fusion.3 = bf16[256,5120]{1,0:T(8,128)(2,1)S(1)} fusion(bf16[3456,5120]{1,0:T(8,128)(2,1)} %param.21, f32[256,3456]{1,0:T(8,128)} %fusion.72, bf16[256,5120]{1,0:T(8,128)(2,1)} %copy-done.28, bf16[5120,3456]{1,0:T(8,128)(2,1)} %param.20), kind=kOutput, calls=%fused_computation.3 | convolution fusion | flops 18126012416 | bytes 79560704 | tf_op jit(solution)/shard_map/dot_general | solution.py:32
  451.8 1.7 fusion.52
  453.5 3.6 collective-permute-start.33
  457.1 3.3 collective-permute-start.37
  463.3 18.7 %fusion.73 = f32[256,3456]{1,0:T(8,128)} fusion(bf16[256,5120]{1,0:T(8,128)(2,1)S(1)} %constant_dynamic-update-slice_fusion.10, bf16[5120,3456]{1,0:T(8,128)(2,1)} %param.19), kind=kOutput, calls=%fused_computation.136 | convolution fusion | flops 9059696640 | bytes 41549824 | tf_op jit(solution)/shard_map/dot_general | solution.py:32
  482.0 32.5 %collective-permute-done.36 = bf16[128,5120]{1,0:T(8,128)(2,1)S(1)} collective-permute-done((bf16[128,5120]{1,0:T(8,128)(2,1)S(1)}, bf16[128,5120]{1,0:T(8,128)(2,1)S(1)}, u32[]{:S(2)}, u32[]{:S(2)}) %collective-permute-start.36) | collective-permute-done | bytes 1310752 | tf_op jit(solution)/shard_map/ppermute | solution.py:183
  516.2 17.8 %fusion.74 = f32[256,3456]{1,0:T(8,128)} fusion(bf16[256,5120]{1,0:T(8,128)(2,1)S(1)} %constant_dynamic-update-slice_fusion.12, bf16[5120,3456]{1,0:T(8,128)(2,1)} %param.19), kind=kOutput, calls=%fused_computation.137 | convolution fusion | flops 9059696640 | bytes 41549824 | tf_op jit(solution)/shard_map/dot_general | solution.py:32
  534.0 34.3 %convolution_convert_fusion.2 = bf16[256,5120]{1,0:T(8,128)(2,1)S(1)} fusion(bf16[3456,5120]{1,0:T(8,128)(2,1)} %param.21, f32[256,3456]{1,0:T(8,128)} %fusion.74, bf16[256,5120]{1,0:T(8,128)(2,1)} %copy-done.26, bf16[5120,3456]{1,0:T(8,128)(2,1)} %param.20), kind=kOutput, calls=%fused_computation.2 | convolution fusion | flops 18126012416 | bytes 79560704 | tf_op jit(solution)/shard_map/dot_general | solution.py:32
  568.3 1.7 fusion.53
  570.0 3.2 collective-permute-start.41
  573.2 36.6 %fusion.29 = f32[256,5120]{1,0:T(8,128)} fusion(bf16[3456,5120]{1,0:T(8,128)(2,1)} %param.21, f32[256,3456]{1,0:T(8,128)} %fusion.73, bf16[256,5120]{1,0:T(8,128)(2,1)} %copy-done.25, bf16[5120,3456]{1,0:T(8,128)(2,1)} %param.20), kind=kOutput, calls=%fused_computation.56 | convolution fusion | flops 18124701696 | bytes 82182144 | tf_op jit(solution)/shard_map/dot_general | solution.py:32
  609.9 4.6 fusion.26
  614.5 3.2 collective-permute-start.42
  617.7 16.5 %fusion.34 = f32[256,5120]{1,0:T(8,128)S(1)} fusion(bf16[3456,5120]{1,0:T(8,128)(2,1)} %param.21, bf16[256,3456]{1,0:T(8,128)(2,1)} %fusion.clone.4), kind=kOutput, calls=%fused_computation.61 | convolution fusion | flops 9059696640 | bytes 42401792 | tf_op jit(solution)/shard_map/dot_general | solution.py:32
  634.2 8.3 %collective-permute-done.39 = bf16[128,5120]{1,0:T(8,128)(2,1)} collective-permute-done((bf16[128,5120]{1,0:T(8,128)(2,1)}, bf16[128,5120]{1,0:T(8,128)(2,1)}, u32[]{:S(2)}, u32[]{:S(2)}) %collective-permute-start.39) | collective-permute-done | bytes 1310752 | tf_op jit(solution)/shard_map/ppermute | solution.py:183
  642.5 3.7 fusion.18
  (172 shorter events, 44.3 us)
Async XLA Ops:
  0.0 9.3 %copy-start.10 = (bf16[256,5120]{1,0:T(8,128)(2,1)S(1)}, bf16[256,5120]{1,0:T(8,128)(2,1)}, u32[]{:S(2)}) copy-start(bf16[256,5120]{1,0:T(8,128)(2,1)} %param.11) | copy-start | bytes 7864324
  0.0 30.3 %collective-permute-start.6 = (s32[256]{0:T(256)}, s32[256]{0:T(256)S(1)}, u32[]{:S(2)}, u32[]{:S(2)}) collective-permute-start(s32[256]{0:T(256)} %param.12), channel_id=1, source_target_pairs={{0,8},{8,16},{16,24},{24,0},{1,9},{9,17},{17,25},{25,1},{2,10},{10... | collective-permute-start | bytes 3080 | tf_op jit(solution)/shard_map/ppermute | solution.py:183
  2.1 28.2 %collective-permute-start.7 = (s32[256]{0:T(256)}, s32[256]{0:T(256)S(1)}, u32[]{:S(2)}, u32[]{:S(2)}) collective-permute-start(s32[256]{0:T(256)} %param.12), channel_id=1, source_target_pairs={{0,24},{8,0},{16,8},{24,16},{1,25},{9,1},{17,9},{25,17},{2,26},{10... | collective-permute-start | bytes 3080 | tf_op jit(solution)/shard_map/ppermute | solution.py:183
  4.7 25.6 %collective-permute-start.14 = (s32[256]{0:T(256)}, s32[256]{0:T(256)S(1)}, u32[]{:S(2)}, u32[]{:S(2)}) collective-permute-start(s32[256]{0:T(256)} %param.12), channel_id=1, source_target_pairs={{0,16},{8,24},{16,0},{24,8},{1,17},{9,25},{17,1},{25,9},{2,18},{10... | collective-permute-start | bytes 3080 | tf_op jit(solution)/shard_map/ppermute | solution.py:183
  11.7 41.0 %collective-permute-start.19 = (bf16[128,5120]{1,0:T(8,128)(2,1)}, bf16[128,5120]{1,0:T(8,128)(2,1)S(1)}, u32[]{:S(2)}, u32[]{:S(2)}) collective-permute-start(bf16[128,5120]{1,0:T(8,128)(2,1)} %get-tuple-element.20), channel_id=1, source_target_pairs={{0,24},{8,0},{16,8},{24,16},{1,25},{9,1},{17,9},{25,17},{2,26},{10... | collective-permute-start | bytes 3932168 | tf_op jit(solution)/shard_map/ppermute | solution.py:183
  12.3 40.5 %collective-permute-start.20 = (bf16[128,5120]{1,0:T(8,128)(2,1)}, bf16[128,5120]{1,0:T(8,128)(2,1)}, u32[]{:S(2)}, u32[]{:S(2)}) collective-permute-start(bf16[128,5120]{1,0:T(8,128)(2,1)} %get-tuple-element.19), channel_id=1, source_target_pairs={{0,8},{8,16},{16,24},{24,0},{1,9},{9,17},{17,25},{25,1},{2,10},{10... | collective-permute-start | bytes 3932168 | tf_op jit(solution)/shard_map/ppermute | solution.py:183
  15.5 7.7 %copy-start.34 = (bf16[5120,1280]{1,0:T(8,128)(2,1)S(1)}, bf16[5120,1280]{1,0:T(8,128)(2,1)}, u32[]{:S(2)}) copy-start(bf16[5120,1280]{1,0:T(8,128)(2,1)} %param.15) | copy-start | bytes 39321604
  23.1 6.6 %copy-start.33 = (s32[256]{0:T(256)S(1)}, s32[256]{0:T(256)}, u32[]{:S(2)}) copy-start(s32[256]{0:T(256)} %param.12) | copy-start | bytes 3076
  23.1 6.6 %copy-start.32 = (bf16[5120]{0:T(1024)(128)(2,1)S(1)}, bf16[5120]{0:T(1024)(128)(2,1)}, u32[]{:S(2)}) copy-start(bf16[5120]{0:T(1024)(128)(2,1)} %param.14) | copy-start | bytes 30724
  35.8 9.4 %collective-permute-start = (bf16[256,512]{1,0:T(8,128)(2,1)}, bf16[256,512]{1,0:T(8,128)(2,1)S(1)}, u32[]{:S(2)}, u32[]{:S(2)}) collective-permute-start(bf16[256,512]{1,0:T(8,128)(2,1)} %kv_finish.4), channel_id=1, source_target_pairs={{0,2},{1,3},{2,4},{3,5},{4,6},{5,7},{6,0},{7,1},{8,10},{9,11},{10,... | collective-permute-start | bytes 786440 | tf_op jit(solution)/shard_map/ppermute | solution.py:186
  35.9 13.8 %collective-permute-start.1 = (bf16[256,512]{1,0:T(8,128)(2,1)}, bf16[256,512]{1,0:T(8,128)(2,1)S(1)}, u32[]{:S(2)}, u32[]{:S(2)}) collective-permute-start(bf16[256,512]{1,0:T(8,128)(2,1)} %kv_finish.4), channel_id=1, source_target_pairs={{0,6},{1,7},{2,0},{3,1},{4,2},{5,3},{6,4},{7,5},{8,14},{9,15},{10,... | collective-permute-start | bytes 786440 | tf_op jit(solution)/shard_map/ppermute | solution.py:186
  37.8 13.8 %collective-permute-start.2 = (bf16[256,512]{1,0:T(8,128)(2,1)}, bf16[256,512]{1,0:T(8,128)(2,1)S(1)}, u32[]{:S(2)}, u32[]{:S(2)}) collective-permute-start(bf16[256,512]{1,0:T(8,128)(2,1)} %kv_finish.4), channel_id=1, source_target_pairs={{0,4},{1,5},{2,6},{3,7},{4,0},{5,1},{6,2},{7,3},{8,12},{9,13},{10,... | collective-permute-start | bytes 786440 | tf_op jit(solution)/shard_map/ppermute | solution.py:186
  45.2 28.3 %collective-permute-start.4 = (bf16[128,5120]{1,0:T(8,128)(2,1)}, bf16[128,5120]{1,0:T(8,128)(2,1)}, u32[]{:S(2)}, u32[]{:S(2)}) collective-permute-start(bf16[128,5120]{1,0:T(8,128)(2,1)} %get-tuple-element.20), channel_id=1, source_target_pairs={{0,8},{8,16},{16,24},{24,0},{1,9},{9,17},{17,25},{25,1},{2,10},{10... | collective-permute-start | bytes 3932168 | tf_op jit(solution)/shard_map/ppermute | solution.py:183
  49.6 25.2 %collective-permute-start.5 = (bf16[128,5120]{1,0:T(8,128)(2,1)}, bf16[128,5120]{1,0:T(8,128)(2,1)}, u32[]{:S(2)}, u32[]{:S(2)}) collective-permute-start(bf16[128,5120]{1,0:T(8,128)(2,1)} %get-tuple-element.19), channel_id=1, source_target_pairs={{0,24},{8,0},{16,8},{24,16},{1,25},{9,1},{17,9},{25,17},{2,26},{10... | collective-permute-start | bytes 3932168 | tf_op jit(solution)/shard_map/ppermute | solution.py:183
  62.6 66.4 %collective-permute-start.21 = (bf16[256,512]{1,0:T(8,128)(2,1)}, bf16[256,512]{1,0:T(8,128)(2,1)S(1)}, u32[]{:S(2)}, u32[]{:S(2)}) collective-permute-start(bf16[256,512]{1,0:T(8,128)(2,1)} %kv_finish.7), channel_id=1, source_target_pairs={{0,2},{1,3},{2,4},{3,5},{4,6},{5,7},{6,0},{7,1},{8,10},{9,11},{10,... | collective-permute-start | bytes 786440 | tf_op jit(solution)/shard_map/ppermute | solution.py:186
  62.6 70.2 %collective-permute-start.22 = (bf16[256,512]{1,0:T(8,128)(2,1)}, bf16[256,512]{1,0:T(8,128)(2,1)S(1)}, u32[]{:S(2)}, u32[]{:S(2)}) collective-permute-start(bf16[256,512]{1,0:T(8,128)(2,1)} %kv_finish.7), channel_id=1, source_target_pairs={{0,6},{1,7},{2,0},{3,1},{4,2},{5,3},{6,4},{7,5},{8,14},{9,15},{10,... | collective-permute-start | bytes 786440 | tf_op jit(solution)/shard_map/ppermute | solution.py:186
  64.8 69.4 %collective-permute-start.23 = (bf16[256,512]{1,0:T(8,128)(2,1)}, bf16[256,512]{1,0:T(8,128)(2,1)S(1)}, u32[]{:S(2)}, u32[]{:S(2)}) collective-permute-start(bf16[256,512]{1,0:T(8,128)(2,1)} %kv_finish.7), channel_id=1, source_target_pairs={{0,4},{1,5},{2,6},{3,7},{4,0},{5,1},{6,2},{7,3},{8,12},{9,13},{10,... | collective-permute-start | bytes 786440 | tf_op jit(solution)/shard_map/ppermute | solution.py:186
  88.9 27.4 %collective-permute-start.12 = (bf16[128,5120]{1,0:T(8,128)(2,1)}, bf16[128,5120]{1,0:T(8,128)(2,1)}, u32[]{:S(2)}, u32[]{:S(2)}) collective-permute-start(bf16[128,5120]{1,0:T(8,128)(2,1)} %collective-permute-done.4), channel_id=1, source_target_pairs={{0,8},{8,16},{16,24},{24,0},{1,9},{9,17},{17,25},{25,1},{2,10},{10... | collective-permute-start | bytes 3932168 | tf_op jit(solution)/shard_map/ppermute | solution.py:183
  88.9 32.5 %collective-permute-start.13 = (bf16[128,5120]{1,0:T(8,128)(2,1)}, bf16[128,5120]{1,0:T(8,128)(2,1)}, u32[]{:S(2)}, u32[]{:S(2)}) collective-permute-start(bf16[128,5120]{1,0:T(8,128)(2,1)} %collective-permute-done.5), channel_id=1, source_target_pairs={{0,24},{8,0},{16,8},{24,16},{1,25},{9,1},{17,9},{25,17},{2,26},{10... | collective-permute-start | bytes 3932168 | tf_op jit(solution)/shard_map/ppermute | solution.py:183
  116.3 18.5 %collective-permute-start.10 = (bf16[256,512]{1,0:T(8,128)(2,1)}, bf16[256,512]{1,0:T(8,128)(2,1)}, u32[]{:S(2)}, u32[]{:S(2)}) collective-permute-start(bf16[256,512]{1,0:T(8,128)(2,1)} %kv_finish.5), channel_id=1, source_target_pairs={{0,4},{1,5},{2,6},{3,7},{4,0},{5,1},{6,2},{7,3},{8,12},{9,13},{10,... | collective-permute-start | bytes 786440 | tf_op jit(solution)/shard_map/ppermute | solution.py:186
  121.3 14.8 %collective-permute-start.8 = (bf16[256,512]{1,0:T(8,128)(2,1)}, bf16[256,512]{1,0:T(8,128)(2,1)}, u32[]{:S(2)}, u32[]{:S(2)}) collective-permute-start(bf16[256,512]{1,0:T(8,128)(2,1)} %kv_finish.5), channel_id=1, source_target_pairs={{0,2},{1,3},{2,4},{3,5},{4,6},{5,7},{6,0},{7,1},{8,10},{9,11},{10,... | collective-permute-start | bytes 786440 | tf_op jit(solution)/shard_map/ppermute | solution.py:186
  123.1 5.8 copy-start.23
  128.9 7.1 %copy-start.29 = (bf16[256,512]{1,0:T(8,128)(2,1)S(1)}, bf16[256,512]{1,0:T(8,128)(2,1)}, u32[]{:S(2)}) copy-start(bf16[256,512]{1,0:T(8,128)(2,1)} %kv_finish.7) | copy-start | bytes 786436
  128.9 13.0 %collective-permute-start.9 = (bf16[256,512]{1,0:T(8,128)(2,1)}, bf16[256,512]{1,0:T(8,128)(2,1)}, u32[]{:S(2)}, u32[]{:S(2)}) collective-permute-start(bf16[256,512]{1,0:T(8,128)(2,1)} %kv_finish.5), channel_id=1, source_target_pairs={{0,6},{1,7},{2,0},{3,1},{4,2},{5,3},{6,4},{7,5},{8,14},{9,15},{10,... | collective-permute-start | bytes 786440 | tf_op jit(solution)/shard_map/ppermute | solution.py:186
  132.7 14.8 %copy-start.30 = (bf16[256,512]{1,0:T(8,128)(2,1)S(1)}, bf16[256,512]{1,0:T(8,128)(2,1)}, u32[]{:S(2)}) copy-start(bf16[256,512]{1,0:T(8,128)(2,1)} %kv_finish.6) | copy-start | bytes 786436
  132.8 10.5 %collective-permute-start.15 = (bf16[256,512]{1,0:T(8,128)(2,1)}, bf16[256,512]{1,0:T(8,128)(2,1)S(1)}, u32[]{:S(2)}, u32[]{:S(2)}) collective-permute-start(bf16[256,512]{1,0:T(8,128)(2,1)} %kv_finish.6), channel_id=1, source_target_pairs={{0,2},{1,3},{2,4},{3,5},{4,6},{5,7},{6,0},{7,1},{8,10},{9,11},{10,... | collective-permute-start | bytes 786440 | tf_op jit(solution)/shard_map/ppermute | solution.py:186
  134.2 13.3 %collective-permute-start.16 = (bf16[256,512]{1,0:T(8,128)(2,1)}, bf16[256,512]{1,0:T(8,128)(2,1)S(1)}, u32[]{:S(2)}, u32[]{:S(2)}) collective-permute-start(bf16[256,512]{1,0:T(8,128)(2,1)} %kv_finish.6), channel_id=1, source_target_pairs={{0,6},{1,7},{2,0},{3,1},{4,2},{5,3},{6,4},{7,5},{8,14},{9,15},{10,... | collective-permute-start | bytes 786440 | tf_op jit(solution)/shard_map/ppermute | solution.py:186
  134.8 12.7 %collective-permute-start.17 = (bf16[256,512]{1,0:T(8,128)(2,1)}, bf16[256,512]{1,0:T(8,128)(2,1)S(1)}, u32[]{:S(2)}, u32[]{:S(2)}) collective-permute-start(bf16[256,512]{1,0:T(8,128)(2,1)} %kv_finish.6), channel_id=1, source_target_pairs={{0,4},{1,5},{2,6},{3,7},{4,0},{5,1},{6,2},{7,3},{8,12},{9,13},{10,... | collective-permute-start | bytes 786440 | tf_op jit(solution)/shard_map/ppermute | solution.py:186
  136.1 11.6 %copy-start.24 = (bf16[256,5120]{1,0:T(8,128)(2,1)S(1)}, bf16[256,5120]{1,0:T(8,128)(2,1)}, u32[]{:S(2)}) copy-start(bf16[256,5120]{1,0:T(8,128)(2,1)} %copy-done.23) | copy-start | bytes 7864324
  136.2 18.4 %collective-permute-start.3 = (bf16[1024,512]{1,0:T(8,128)(2,1)S(1)}, bf16[1024,512]{1,0:T(8,128)(2,1)S(1)}, u32[]{:S(2)}, u32[]{:S(2)}) collective-permute-start(bf16[1024,512]{1,0:T(8,128)(2,1)S(1)} %pad_maximum_fusion.9.rest_0_), channel_id=1, source_target_pairs={{0,1},{1,0},{2,3},{3,2},{4,5},{5,4},{6,7},{7,6},{8,9},{9,8},{10,11... | collective-permute-start | bytes 3145736 | tf_op jit(solution)/shard_map/ppermute | solution.py:189
  142.0 12.6 %collective-permute-start.24 = (bf16[1024,512]{1,0:T(8,128)(2,1)S(1)}, bf16[1024,512]{1,0:T(8,128)(2,1)S(1)}, u32[]{:S(2)}, u32[]{:S(2)}) collective-permute-start(bf16[1024,512]{1,0:T(8,128)(2,1)S(1)} %pad_maximum_fusion.12.rest_6_), channel_id=1, source_target_pairs={{0,1},{1,0},{2,3},{3,2},{4,5},{5,4},{6,7},{7,6},{8,9},{9,8},{10,11... | collective-permute-start | bytes 3145736 | tf_op jit(solution)/shard_map/ppermute | solution.py:189
  143.3 11.3 %collective-permute-start.11 = (bf16[1024,512]{1,0:T(8,128)(2,1)S(1)}, bf16[1024,512]{1,0:T(8,128)(2,1)S(1)}, u32[]{:S(2)}, u32[]{:S(2)}) collective-permute-start(bf16[1024,512]{1,0:T(8,128)(2,1)S(1)} %pad_maximum_fusion.10.rest_2_), channel_id=1, source_target_pairs={{0,1},{1,0},{2,3},{3,2},{4,5},{5,4},{6,7},{7,6},{8,9},{9,8},{10,11... | collective-permute-start | bytes 3145736 | tf_op jit(solution)/shard_map/ppermute | solution.py:189
  147.6 7.0 %copy-start.3 = (f32[256,128]{1,0:T(8,128)S(1)}, f32[256,128]{1,0:T(8,128)}, u32[]{:S(2)}) copy-start(f32[256,128]{1,0:T(8,128)} %pad_maximum_fusion.16.s_ref) | copy-start | bytes 393220
  147.6 7.0 %copy-start.7 = (f32[256,128]{1,0:T(8,128)S(1)}, f32[256,128]{1,0:T(8,128)}, u32[]{:S(2)}) copy-start(f32[256,128]{1,0:T(8,128)} %pad_maximum_fusion.15.c_ref) | copy-start | bytes 393220
  147.6 7.0 %copy-start.8 = (f32[256,1280]{1,0:T(8,128)S(1)}, f32[256,1280]{1,0:T(8,128)}, u32[]{:S(2)}) copy-start(f32[256,1280]{1,0:T(8,128)} %fusion.68.q_ref) | copy-start | bytes 3932164
  147.6 7.0 %collective-permute-start.18 = (bf16[1024,512]{1,0:T(8,128)(2,1)S(1)}, bf16[1024,512]{1,0:T(8,128)(2,1)S(1)}, u32[]{:S(2)}, u32[]{:S(2)}) collective-permute-start(bf16[1024,512]{1,0:T(8,128)(2,1)S(1)} %pad_maximum_fusion.11.rest_4_), channel_id=1, source_target_pairs={{0,1},{1,0},{2,3},{3,2},{4,5},{5,4},{6,7},{7,6},{8,9},{9,8},{10,11... | collective-permute-start | bytes 3145736 | tf_op jit(solution)/shard_map/ppermute | solution.py:189
  198.4 135.9 %collective-permute-start.25 = (bf16[128,5120]{1,0:T(8,128)(2,1)S(1)}, bf16[128,5120]{1,0:T(8,128)(2,1)S(1)}, u32[]{:S(2)}, u32[]{:S(2)}) collective-permute-start(bf16[128,5120]{1,0:T(8,128)(2,1)S(1)} %get-tuple-element.25), channel_id=1, source_target_pairs={{0,24},{8,0},{16,8},{24,16},{1,25},{9,1},{17,9},{25,17},{2,26},{10... | collective-permute-start | bytes 3932168 | tf_op jit(solution)/shard_map/ppermute | solution.py:183
  199.7 134.7 %collective-permute-start.28 = (bf16[128,5120]{1,0:T(8,128)(2,1)S(1)}, bf16[128,5120]{1,0:T(8,128)(2,1)S(1)}, u32[]{:S(2)}, u32[]{:S(2)}) collective-permute-start(bf16[128,5120]{1,0:T(8,128)(2,1)S(1)} %get-tuple-element.26), channel_id=1, source_target_pairs={{0,8},{8,16},{16,24},{24,0},{1,9},{9,17},{17,25},{25,1},{2,10},{10... | collective-permute-start | bytes 3932168 | tf_op jit(solution)/shard_map/ppermute | solution.py:183
  244.1 44.5 %collective-permute-start.26 = (bf16[128,5120]{1,0:T(8,128)(2,1)S(1)}, bf16[128,5120]{1,0:T(8,128)(2,1)S(1)}, u32[]{:S(2)}, u32[]{:S(2)}) collective-permute-start(bf16[128,5120]{1,0:T(8,128)(2,1)S(1)} %get-tuple-element.27), channel_id=1, source_target_pairs={{0,8},{8,16},{16,24},{24,0},{1,9},{9,17},{17,25},{25,1},{2,10},{10... | collective-permute-start | bytes 3932168 | tf_op jit(solution)/shard_map/ppermute | solution.py:183
  244.2 44.4 %collective-permute-start.29 = (bf16[128,5120]{1,0:T(8,128)(2,1)S(1)}, bf16[128,5120]{1,0:T(8,128)(2,1)S(1)}, u32[]{:S(2)}, u32[]{:S(2)}) collective-permute-start(bf16[128,5120]{1,0:T(8,128)(2,1)S(1)} %get-tuple-element.28), channel_id=1, source_target_pairs={{0,24},{8,0},{16,8},{24,16},{1,25},{9,1},{17,9},{25,17},{2,26},{10... | collective-permute-start | bytes 3932168 | tf_op jit(solution)/shard_map/ppermute | solution.py:183
  288.6 4.4 copy-start
  288.6 4.4 copy-start.4
  288.6 4.4 copy-start.9
  289.5 44.9 %collective-permute-start.27 = (bf16[128,5120]{1,0:T(8,128)(2,1)S(1)}, bf16[128,5120]{1,0:T(8,128)(2,1)S(1)}, u32[]{:S(2)}, u32[]{:S(2)}) collective-permute-start(bf16[128,5120]{1,0:T(8,128)(2,1)S(1)} %get-tuple-element.17), channel_id=1, source_target_pairs={{0,8},{8,16},{16,24},{24,0},{1,9},{9,17},{17,25},{25,1},{2,10},{10... | collective-permute-start | bytes 3932168 | tf_op jit(solution)/shard_map/ppermute | solution.py:183
  289.6 44.8 %collective-permute-start.30 = (bf16[128,5120]{1,0:T(8,128)(2,1)S(1)}, bf16[128,5120]{1,0:T(8,128)(2,1)S(1)}, u32[]{:S(2)}, u32[]{:S(2)}) collective-permute-start(bf16[128,5120]{1,0:T(8,128)(2,1)S(1)} %get-tuple-element.18), channel_id=1, source_target_pairs={{0,24},{8,0},{16,8},{24,16},{1,25},{9,1},{17,9},{25,17},{2,26},{10... | collective-permute-start | bytes 3932168 | tf_op jit(solution)/shard_map/ppermute | solution.py:183
  327.6 6.8 %copy-start.11 = (bf16[256,5120]{1,0:T(8,128)(2,1)S(1)}, bf16[256,5120]{1,0:T(8,128)(2,1)}, u32[]{:S(2)}) copy-start(bf16[256,5120]{1,0:T(8,128)(2,1)} %param.11) | copy-start | bytes 7864324
  338.7 42.5 %collective-permute-start.31 = (bf16[128,5120]{1,0:T(8,128)(2,1)}, bf16[128,5120]{1,0:T(8,128)(2,1)S(1)}, u32[]{:S(2)}, u32[]{:S(2)}) collective-permute-start(bf16[128,5120]{1,0:T(8,128)(2,1)} %get-tuple-element.29), channel_id=1, source_target_pairs={{0,8},{8,16},{16,24},{24,0},{1,9},{9,17},{17,25},{25,1},{2,10},{10... | collective-permute-start | bytes 3932168 | tf_op jit(solution)/shard_map/ppermute | solution.py:183
  338.7 118.4 %collective-permute-start.34 = (bf16[128,5120]{1,0:T(8,128)(2,1)}, bf16[128,5120]{1,0:T(8,128)(2,1)}, u32[]{:S(2)}, u32[]{:S(2)}) collective-permute-start(bf16[128,5120]{1,0:T(8,128)(2,1)} %get-tuple-element.29), channel_id=1, source_target_pairs={{0,24},{8,0},{16,8},{24,16},{1,25},{9,1},{17,9},{25,17},{2,26},{10... | collective-permute-start | bytes 3932168 | tf_op jit(solution)/shard_map/ppermute | solution.py:183
  341.9 55.0 %collective-permute-start.32 = (bf16[128,5120]{1,0:T(8,128)(2,1)}, bf16[128,5120]{1,0:T(8,128)(2,1)S(1)}, u32[]{:S(2)}, u32[]{:S(2)}) collective-permute-start(bf16[128,5120]{1,0:T(8,128)(2,1)} %get-tuple-element.30), channel_id=1, source_target_pairs={{0,24},{8,0},{16,8},{24,16},{1,25},{9,1},{17,9},{25,17},{2,26},{10... | collective-permute-start | bytes 3932168 | tf_op jit(solution)/shard_map/ppermute | solution.py:183
  342.0 119.9 %collective-permute-start.35 = (bf16[128,5120]{1,0:T(8,128)(2,1)}, bf16[128,5120]{1,0:T(8,128)(2,1)}, u32[]{:S(2)}, u32[]{:S(2)}) collective-permute-start(bf16[128,5120]{1,0:T(8,128)(2,1)} %get-tuple-element.30), channel_id=1, source_target_pairs={{0,8},{8,16},{16,24},{24,0},{1,9},{9,17},{17,25},{25,1},{2,10},{10... | collective-permute-start | bytes 3932168 | tf_op jit(solution)/shard_map/ppermute | solution.py:183
  381.2 15.8 %copy-start.19 = (bf16[128,5120]{1,0:T(8,128)(2,1)}, bf16[128,5120]{1,0:T(8,128)(2,1)S(1)}, u32[]{:S(2)}) copy-start(bf16[128,5120]{1,0:T(8,128)(2,1)S(1)} %collective-permute-done.31) | copy-start | bytes 3932164
  451.8 5.3 copy-start.20
  451.8 5.3 copy-start.22
  453.5 180.7 %collective-permute-start.33 = (bf16[128,5120]{1,0:T(8,128)(2,1)}, bf16[128,5120]{1,0:T(8,128)(2,1)}, u32[]{:S(2)}, u32[]{:S(2)}) collective-permute-start(bf16[128,5120]{1,0:T(8,128)(2,1)} %get-tuple-element.21), channel_id=1, source_target_pairs={{0,24},{8,0},{16,8},{24,16},{1,25},{9,1},{17,9},{25,17},{2,26},{10... | collective-permute-start | bytes 3932168 | tf_op jit(solution)/shard_map/ppermute | solution.py:183
  457.1 177.1 %collective-permute-start.40 = (bf16[128,5120]{1,0:T(8,128)(2,1)}, bf16[128,5120]{1,0:T(8,128)(2,1)}, u32[]{:S(2)}, u32[]{:S(2)}) collective-permute-start(bf16[128,5120]{1,0:T(8,128)(2,1)} %get-tuple-element.22), channel_id=1, source_target_pairs={{0,8},{8,16},{16,24},{24,0},{1,9},{9,17},{17,25},{25,1},{2,10},{10... | collective-permute-start | bytes 3932168 | tf_op jit(solution)/shard_map/ppermute | solution.py:183
  457.1 57.4 %collective-permute-start.36 = (bf16[128,5120]{1,0:T(8,128)(2,1)S(1)}, bf16[128,5120]{1,0:T(8,128)(2,1)S(1)}, u32[]{:S(2)}, u32[]{:S(2)}) collective-permute-start(bf16[128,5120]{1,0:T(8,128)(2,1)S(1)} %copy-done.20), channel_id=1, source_target_pairs={{0,8},{8,16},{16,24},{24,0},{1,9},{9,17},{17,25},{25,1},{2,10},{10... | collective-permute-start | bytes 3932168 | tf_op jit(solution)/shard_map/ppermute | solution.py:183
  457.1 57.5 %collective-permute-start.37 = (bf16[128,5120]{1,0:T(8,128)(2,1)S(1)}, bf16[128,5120]{1,0:T(8,128)(2,1)S(1)}, u32[]{:S(2)}, u32[]{:S(2)}) collective-permute-start(bf16[128,5120]{1,0:T(8,128)(2,1)S(1)} %copy-done.22), channel_id=1, source_target_pairs={{0,24},{8,0},{16,8},{24,16},{1,25},{9,1},{17,9},{25,17},{2,26},{10... | collective-permute-start | bytes 3932168 | tf_op jit(solution)/shard_map/ppermute | solution.py:183
  463.3 18.8 %copy-start.25 = (bf16[256,5120]{1,0:T(8,128)(2,1)}, bf16[256,5120]{1,0:T(8,128)(2,1)S(1)}, u32[]{:S(2)}) copy-start(bf16[256,5120]{1,0:T(8,128)(2,1)S(1)} %constant_dynamic-update-slice_fusion.10) | copy-start | bytes 7864324
  570.0 39.9 %collective-permute-start.38 = (bf16[128,5120]{1,0:T(8,128)(2,1)}, bf16[128,5120]{1,0:T(8,128)(2,1)S(1)}, u32[]{:S(2)}, u32[]{:S(2)}) collective-permute-start(bf16[128,5120]{1,0:T(8,128)(2,1)} %get-tuple-element.23), channel_id=1, source_target_pairs={{0,8},{8,16},{16,24},{24,0},{1,9},{9,17},{17,25},{25,1},{2,10},{10... | collective-permute-start | bytes 3932168 | tf_op jit(solution)/shard_map/ppermute | solution.py:183
  570.0 39.9 %collective-permute-start.41 = (bf16[128,5120]{1,0:T(8,128)(2,1)}, bf16[128,5120]{1,0:T(8,128)(2,1)}, u32[]{:S(2)}, u32[]{:S(2)}) collective-permute-start(bf16[128,5120]{1,0:T(8,128)(2,1)} %get-tuple-element.24), channel_id=1, source_target_pairs={{0,24},{8,0},{16,8},{24,16},{1,25},{9,1},{17,9},{25,17},{2,26},{10... | collective-permute-start | bytes 3932168 | tf_op jit(solution)/shard_map/ppermute | solution.py:183
  614.5 28.0 %collective-permute-start.39 = (bf16[128,5120]{1,0:T(8,128)(2,1)}, bf16[128,5120]{1,0:T(8,128)(2,1)}, u32[]{:S(2)}, u32[]{:S(2)}) collective-permute-start(bf16[128,5120]{1,0:T(8,128)(2,1)} %get-tuple-element.15), channel_id=1, source_target_pairs={{0,8},{8,16},{16,24},{24,0},{1,9},{9,17},{17,25},{25,1},{2,10},{10... | collective-permute-start | bytes 3932168 | tf_op jit(solution)/shard_map/ppermute | solution.py:183
  614.5 28.0 %copy-start.13 = (bf16[128,5120]{1,0:T(8,128)(2,1)S(1)}, bf16[128,5120]{1,0:T(8,128)(2,1)}, u32[]{:S(2)}) copy-start(bf16[128,5120]{1,0:T(8,128)(2,1)} %copy-done.12) | copy-start | bytes 3932164
  614.5 28.0 %copy-start.15 = (bf16[128,5120]{1,0:T(8,128)(2,1)S(1)}, bf16[128,5120]{1,0:T(8,128)(2,1)}, u32[]{:S(2)}) copy-start(bf16[128,5120]{1,0:T(8,128)(2,1)} %copy-done.14) | copy-start | bytes 3932164
  614.5 28.0 %collective-permute-start.42 = (bf16[128,5120]{1,0:T(8,128)(2,1)S(1)}, bf16[128,5120]{1,0:T(8,128)(2,1)}, u32[]{:S(2)}, u32[]{:S(2)}) collective-permute-start(bf16[128,5120]{1,0:T(8,128)(2,1)S(1)} %get-tuple-element.16), channel_id=1, source_target_pairs={{0,24},{8,0},{16,8},{24,16},{1,25},{9,1},{17,9},{25,17},{2,26},{10... | collective-permute-start | bytes 3932168 | tf_op jit(solution)/shard_map/ppermute | solution.py:183
  (14 other events, 32.9 us)

commit v2 on v1

v2 whole, which is shorter than its diff:
```python
import functools
import math

import jax
import jax.numpy as jnp
from jax import lax
from jax.experimental import pallas as pl
from jax.experimental.pallas import tpu as pltpu
from jax.sharding import PartitionSpec as P

DH = 128
EPS = 1e-5
THETA = 500000.0
NEG = -1e30


def rms_norm(v, g):
    vf = v.astype(jnp.float32)
    inv = lax.rsqrt(jnp.mean(vf * vf, axis=-1, keepdims=True) + EPS)
    return (vf * inv * g.astype(jnp.float32)).astype(jnp.bfloat16)


def tables(p):
    freq = 1.0 / (THETA ** (jnp.arange(0, DH, 2, dtype=jnp.float32) / DH))
    ang = p.astype(jnp.float32)[:, None] * freq
    c = jnp.cos(ang)
    s = jnp.sin(ang)
    return jnp.concatenate([c, c], axis=1), jnp.concatenate([-s, s], axis=1)


def dot32(a, b):
    return jnp.dot(a, b, preferred_element_type=jnp.float32)


def chunk(n, most):
    c = most
    while n % c:
        c = c // 2
    return c


def proj_kernel(roped, lo_ref, hi_ref, c_ref, s_ref, *rest):
    n = len(roped)
    ws, o_ref, acc = rest[:n], rest[n], rest[n + 1]
    i = pl.program_id(0)
    a = jnp.concatenate([lo_ref[...], hi_ref[...]], axis=0)

    @pl.when(i == 0)
    def _():
        acc[...] = jnp.zeros_like(acc)

    at = 0
    for w in ws:
        wide = w.shape[1]
        acc[:, at:at + wide] += dot32(a, w[...])
        at += wide

    @pl.when(i == pl.num_programs(0) - 1)
    def _():
        c = c_ref[...]
        s = s_ref[...]
        at = 0
        for w, rot in zip(ws, roped):
            for _ in range(w.shape[1] // DH):
                u = acc[:, at:at + DH]
                if rot:
                    u = u * c + pltpu.roll(u, DH // 2, 1) * s
                o_ref[:, at:at + DH] = u.astype(jnp.bfloat16)
                at += DH


def project(lo, hi, c, s, ws, roped):
    h, depth = lo.shape
    wide = sum(w.shape[1] for w in ws)
    kb = chunk(depth, 1024)
    tab = pl.BlockSpec((2 * h, DH), lambda i: (0, 0))
    act = pl.BlockSpec((h, kb), lambda i: (0, i))
    return pl.pallas_call(
        functools.partial(proj_kernel, roped),
        out_shape=jax.ShapeDtypeStruct((2 * h, wide), jnp.bfloat16),
        grid=(depth // kb,),
        in_specs=[act, act, tab, tab] + [pl.BlockSpec((kb, w.shape[1]), lambda i: (i, 0)) for w in ws],
        out_specs=pl.BlockSpec((2 * h, wide), lambda i: (0, 0)),
        scratch_shapes=[pltpu.VMEM((2 * h, wide), jnp.float32)],
        compiler_params=pltpu.CompilerParams(dimension_semantics=("arbitrary",)),
        cost_estimate=pl.CostEstimate(flops=4 * h * depth * wide, bytes_accessed=2 * depth * (wide + 2 * h), transcendentals=0),
    )(lo, hi, c, s, *ws)


def gate_kernel(lo_ref, hi_ref, w1_ref, w3_ref, o_ref, acc1, acc3):
    i = pl.program_id(0)
    a = jnp.concatenate([lo_ref[...], hi_ref[...]], axis=0)

    @pl.when(i == 0)
    def _():
        acc1[...] = jnp.zeros_like(acc1)
        acc3[...] = jnp.zeros_like(acc3)

    acc1[...] += dot32(a, w1_ref[...])
    acc3[...] += dot32(a, w3_ref[...])

    @pl.when(i == pl.num_programs(0) - 1)
    def _():
        o_ref[...] = (jax.nn.silu(acc1[...]) * acc3[...]).astype(jnp.bfloat16)


def gate(lo, hi, w1, w3):
    h, depth = lo.shape
    wide = w1.shape[1]
    kb = chunk(depth, 512)
    act = pl.BlockSpec((h, kb), lambda i: (0, i))
    wsp = pl.BlockSpec((kb, wide), lambda i: (i, 0))
    return pl.pallas_call(
        gate_kernel,
        out_shape=jax.ShapeDtypeStruct((2 * h, wide), jnp.bfloat16),
        grid=(depth // kb,),
        in_specs=[act, act, wsp, wsp],
        out_specs=pl.BlockSpec((2 * h, wide), lambda i: (0, 0)),
        scratch_shapes=[pltpu.VMEM((2 * h, wide), jnp.float32)] * 2,
        compiler_params=pltpu.CompilerParams(dimension_semantics=("arbitrary",)),
        cost_estimate=pl.CostEstimate(flops=8 * h * depth * wide, bytes_accessed=4 * depth * (wide + h), transcendentals=2 * h * wide),
    )(lo, hi, w1, w3)


def down_kernel(a_ref, w_ref, lo_ref, hi_ref):
    h = lo_ref.shape[0]
    y = dot32(a_ref[...], w_ref[...])
    lo_ref[...] = y[:h].astype(lo_ref.dtype)
    hi_ref[...] = y[h:].astype(hi_ref.dtype)


def down(a, w, dtype):
    rows, depth = a.shape
    wide = w.shape[1]
    nb = chunk(wide, 512)
    out = pl.BlockSpec((rows // 2, nb), lambda i: (0, i))
    return pl.pallas_call(
        down_kernel,
        out_shape=[jax.ShapeDtypeStruct((rows // 2, wide), dtype)] * 2,
        grid=(wide // nb,),
        in_specs=[pl.BlockSpec((rows, depth), lambda i: (0, 0)), pl.BlockSpec((depth, nb), lambda i: (0, i))],
        out_specs=[out, out],
        compiler_params=pltpu.CompilerParams(dimension_semantics=("arbitrary",)),
        cost_estimate=pl.CostEstimate(flops=2 * rows * depth * wide, bytes_accessed=2 * depth * (wide + rows), transcendentals=0),
    )(a, w)


LOW = (0, -1, 2, 1)
HIGH = (0, 1, 2, -1)


def attn_kernel(ntp, ncp, bat, info_ref, q_ref, *rest):
    kvs = rest[:8]
    wo_hbm, lo_ref, hi_ref, kv, wo, qs, acc, ms, ls, o, ksem, wsem = rest[8:]
    piece = q_ref.shape[0] // 2
    heads = q_ref.shape[1] // DH
    kvh = kv.shape[1] // (2 * DH)
    grp = heads // kvh
    mrow = grp * piece
    blk = ntp * piece
    npc = 2 * ntp * ncp
    cc = info_ref[0]
    jj = info_ref[1]
    mate = cc + 1 - 2 * lax.rem(cc, 2)
    last = 2 * ncp - 1 - cc

    def owner(s):
        low = s < ncp
        return jnp.where(low, s, 2 * ncp - 1 - s), jnp.where(low, 0, 1)

    def piece_of(c_src, half, b):
        kl = c_src * ntp + lax.rem(jj + LOW[b] + ntp, ntp)
        kh = c_src * ntp + lax.rem(jj + HIGH[b] + ntp, ntp)
        return jnp.where(half == 0, kl, npc - 1 - kh)

    def load(s, z):
        c_src, half = owner(s)
        same = lax.rem(c_src + cc, 2) == 0
        e = lax.rem(c_src - jnp.where(same, cc, mate) + ncp, ncp) // 2
        off = pl.multiple_of((2 * e + half) * piece, piece)
        for b in range(4):
            dst = kv.at[pl.ds(pl.multiple_of(s * blk + b * piece, piece), piece), :]

            @pl.when(same)
            def _():
                pltpu.make_async_copy(kvs[2 * b].at[pl.ds(off, piece), :], dst, ksem.at[s]).start()

            @pl.when(jnp.logical_not(same))
            def _():
                pltpu.make_async_copy(kvs[2 * b + 1].at[pl.ds(off, piece), :], dst, ksem.at[s]).start()
        return z

    lax.fori_loop(0, last + 1, load, 0)
    wcopy = pltpu.make_async_copy(wo_hbm, wo, wsem)
    wcopy.start()

    scale = math.log2(math.e) / math.sqrt(DH)

    def one_half(turn, z):
        half = 1 - turn
        r0 = pl.multiple_of(half * piece, piece)
        ms[...] = jnp.full_like(ms, NEG)
        ls[...] = jnp.zeros_like(ls)
        acc[...] = jnp.zeros_like(acc)
        for h in range(heads):
            qs[h // grp, (h % grp) * piece:(h % grp + 1) * piece, :] = q_ref[pl.ds(r0, piece), h * DH:(h + 1) * DH]
        diag = jnp.where(half == 0, cc, last)

        def step(i, masked):
            k0 = pl.multiple_of(i * blk, blk)

            @pl.when(turn == 0)
            def _():
                dst = kv.at[pl.ds(k0, blk), :]
                pltpu.make_async_copy(dst, dst, ksem.at[i]).wait()

            ss = []
            for g in range(kvh):
                kk = kv[pl.ds(k0, blk), g * DH:(g + 1) * DH]
                ss.append(lax.dot_general(qs[g], kk, (((1,), (1,)), ((), ())), preferred_element_type=jnp.float32))
            if masked:
                c_src, hf = owner(i)
                row = lax.broadcasted_iota(jnp.int32, (mrow, 1), 0)
                row = lax.rem(row, piece) + piece_of(cc, half, bat) * piece
                col = lax.broadcasted_iota(jnp.int32, (1, blk), 1)
                base = jnp.zeros((1, blk), jnp.int32)
                for b in range(4):
                    base = jnp.where(col >= b * piece, (piece_of(c_src, hf, b) - b) * piece, base)
                keep = (col + base) <= row
                ss = [jnp.where(keep, s, NEG) for s in ss]
            for g in range(kvh):
                s = ss[g]
                vv = kv[pl.ds(k0, blk), (kvh + g) * DH:(kvh + g + 1) * DH]
                m_old = ms[g]
                m_new = jnp.maximum(m_old, jnp.max(s, axis=1, keepdims=True))
                alpha = jnp.exp2((m_old - m_new) * scale)
                ms[g] = m_new
                ps = []
                lsum = ls[g] * alpha
                for t in range(blk // DH):
                    pt = jnp.exp2((s[:, t * DH:(t + 1) * DH] - m_new) * scale)
                    lsum = lsum + pt
                    ps.append(pt.astype(jnp.bfloat16))
                ls[g] = lsum
                acc[g] = acc[g] * alpha + dot32(jnp.concatenate(ps, axis=1), vv)

        lax.fori_loop(0, diag, lambda i, y: (step(i, False), y)[1], 0)
        step(diag, True)
        for g in range(kvh):
            og = acc[g] / jnp.sum(ls[g], axis=1, keepdims=True)
            for h in range(grp):
                hh = g * grp + h
                o[pl.ds(r0, piece), hh * DH:(hh + 1) * DH] = og[h * piece:(h + 1) * piece, :].astype(jnp.bfloat16)
        return z

    lax.fori_loop(0, 2, one_half, 0)
    wcopy.wait()
    nb = chunk(wo.shape[1], 512)

    def out(n, z):
        cols = pl.ds(pl.multiple_of(n * nb, nb), nb)
        y = dot32(o[...], wo[:, cols])
        lo_ref[:, cols] = y[:piece].astype(lo_ref.dtype)
        hi_ref[:, cols] = y[piece:].astype(hi_ref.dtype)
        return z

    lax.fori_loop(0, wo.shape[1] // nb, out, 0)


def attend(bat, ntp, ncp, info, q, kvs, wo, dtype):
    rows, width = q.shape
    piece = rows // 2
    kvw = kvs[0].shape[1]
    kvh = kvw // (2 * DH)
    mrow = (width // DH // kvh) * piece
    total = 2 * ntp * ncp * piece
    vm = pl.BlockSpec(memory_space=pltpu.VMEM)
    hbm = pl.BlockSpec(memory_space=pltpu.HBM)
    state = pltpu.VMEM((kvh, mrow, DH), jnp.float32)
    return pl.pallas_call(
        functools.partial(attn_kernel, ntp, ncp, bat),
        out_shape=[jax.ShapeDtypeStruct((piece, wo.shape[1]), dtype)] * 2,
        in_specs=[pl.BlockSpec(memory_space=pltpu.SMEM), vm] + [hbm] * 9,
        out_specs=[vm, vm],
        scratch_shapes=[
            pltpu.VMEM((total, kvw), jnp.bfloat16),
            pltpu.VMEM(wo.shape, jnp.bfloat16),
            pltpu.VMEM((kvh, mrow, DH), jnp.bfloat16),
            state, state, state,
            pltpu.VMEM((rows, width), jnp.bfloat16),
            pltpu.SemaphoreType.DMA((2 * ncp,)),
            pltpu.SemaphoreType.DMA,
        ],
        cost_estimate=pl.CostEstimate(
            flops=2 * 10**10, bytes_accessed=2 * total * kvw + 2 * wo.size, transcendentals=rows * width // DH * total // 2),
    )(info, q, *kvs, wo)


def solution(mesh):
    tok = P(('dp', 'cp', 'tp'), None)
    col = P(None, 'tp')
    row = P('tp', None)
    ntp = mesh.shape['tp']
    ncp = mesh.shape['cp']
    assert ntp == 4 and ncp == 8

    def tshift(v, d):
        return lax.ppermute(v, 'tp', [(i, (i + d) % ntp) for i in range(ntp)])

    def cshift(v, d):
        return lax.ppermute(v, 'cp', [(i, (i + d) % ncp) for i in range(ncp)])

    def cswap(v):
        return lax.ppermute(v, 'cp', [(i, i ^ 1) for i in range(ncp)])

    def cat(u, v):
        return jnp.concatenate([u, v], axis=0)

    def gather(lo, hi):
        p_lo = tshift(lo, 1)
        m_hi = tshift(hi, -1)
        p_hi = tshift(hi, 1)
        m_lo = tshift(lo, -1)
        f_lo = tshift(p_lo, 1)
        f_hi = tshift(m_hi, -1)
        return (p_lo, m_hi), (f_lo, f_hi), (m_lo, p_hi)

    def layer(x, pos, g1, g2, wq, wk, wv, wo, w1, w3, w2):
        n = x.shape[0]
        h = n // 2
        pos_p = tshift(pos, 1)
        pos_m = tshift(pos, -1)
        pos_2 = tshift(pos, 2)
        info = jnp.stack([lax.axis_index('cp'), lax.axis_index('tp')]).astype(jnp.int32)

        lo = rms_norm(x[:h], g1)
        hi = rms_norm(x[h:], g1)
        parts = [(lo, hi)] + list(gather(lo, hi))
        ptab = [pos, cat(pos_p[:h], pos_m[h:]), pos_2, cat(pos_m[:h], pos_p[h:])]
        tabs = [tables(p) for p in ptab]
        qs, kvs = [], []
        for b in range(4):
            kv = project(*parts[b], *tabs[b], (wk, wv), (True, False))
            stack = jnp.concatenate([kv, cshift(kv, -2), cshift(kv, 4), cshift(kv, 2)], axis=0)
            kvs += [stack, cswap(stack)]
            qs.append(project(*parts[b], *tabs[b], (wq,), (True,)))

        def scatter(part):
            y_lo, y_hi = part(1, jnp.bfloat16)
            r1_lo = tshift(y_lo, -1)
            r1_hi = tshift(y_hi, 1)
            y_lo, y_hi = part(2, jnp.bfloat16)
            s_lo = tshift(y_lo, 1)
            s_hi = tshift(y_hi, -1)
            y_lo, y_hi = part(3, jnp.float32)
            y_lo = (y_lo + s_lo.astype(jnp.float32)).astype(jnp.bfloat16)
            y_hi = (y_hi + s_hi.astype(jnp.float32)).astype(jnp.bfloat16)
            r3_lo = tshift(y_lo, 1)
            r3_hi = tshift(y_hi, -1)
            return part(0, jnp.float32), (r1_lo, r1_hi), (r3_lo, r3_hi)

        def total(base, y, r1, r3, i):
            t = base.astype(jnp.float32) + y + r1[i].astype(jnp.float32) + r3[i].astype(jnp.float32)
            return t.astype(jnp.bfloat16)

        y, r1, r3 = scatter(lambda b, t: attend(b, ntp, ncp, info, qs[b], kvs, wo, t))
        h_lo = total(x[:h], y[0], r1, r3, 0)
        h_hi = total(x[h:], y[1], r1, r3, 1)

        lo = rms_norm(h_lo, g2)
        hi = rms_norm(h_hi, g2)
        parts2 = [(lo, hi)] + list(gather(lo, hi))
        hid = []
        for b in range(4):
            hid.append(gate(*parts2[b], w1, w3))

        def part(b, t):
            return down(hid[b], w2, t)

        y, r1, r3 = scatter(part)
        return cat(total(h_lo, y[0], r1, r3, 0), total(h_hi, y[1], r1, r3, 1))

    return jax.shard_map(layer, mesh=mesh, in_specs=(tok, P(('dp', 'cp', 'tp')), P(None), P(None), col, col, col, row, col, col, row),
                         out_specs=tok, check_vma=False)
```

time: 657 us -> 610 us (0.928)
  the two profiles are of different devices: /device:TPU:102 before, /device:TPU:97 now
where the time goes in v2:
time: 610 us; the launch traced here: 600 us
  Pallas kernels  379 us (62%)
  waiting for transfers between devices  110 us (18%)
  starting transfers between devices  62 us (10%)
  other arithmetic  48.2 us (8%)
    pallas_call x4, Pallas kernels, gate(): pl.pallas_call(gate_kernel, out_shape=jax.ShapeDtypeStruct((2 * h, wide),...  125 us
    pallas_call x4, Pallas kernels, attend(): pl.pallas_call(functools.partial(attn_kernel, ntp, ncp, bat), out_shape=[...  110 us
    ppermute x27, waiting for transfers between devices, tshift(): return lax.ppermute(v, 'tp', [(i, (i + d) % ntp) for i in range(ntp)])  108 us
    pallas_call x4, Pallas kernels, down(): pl.pallas_call(down_kernel, out_shape=[jax.ShapeDtypeStruct((rows // 2, w...  77.5 us
    pallas_call x8, Pallas kernels, project(): pl.pallas_call(functools.partial(proj_kernel, roped), out_shape=jax.Shape...  65.8 us
    ppermute x27, starting transfers between devices, tshift(): return lax.ppermute(v, 'tp', [(i, (i + d) % ntp) for i in range(ntp)])  34.6 us
    ppermute x12, starting transfers between devices, cshift(): return lax.ppermute(v, 'cp', [(i, (i + d) % ncp) for i in range(ncp)])  18.3 us
  transfers between devices with their start and end apart: 43, of which 9 were waited for; matrix products, arithmetic and copies ran while one was open for 6% of the time, Pallas kernels for 59%

profile of v2, /device:TPU:97, one launch (start us, length us, event | category | flops | bytes accessed | tf_op | source)
XLA Modules:
  0.0 599.9 jit_solution(252902541585180195)
XLA Ops:
  0.0 2.5 fusion.6
  3.2 2.3 fusion.8
  5.5 2.7 collective-permute-start.4
  8.2 2.5 collective-permute-start.5
  10.7 2.7 collective-permute-start.7
  14.7 24.9 %collective-permute-done.6 = s32[256]{0:T(256)S(1)} collective-permute-done((s32[256]{0:T(256)S(1)}, s32[256]{0:T(256)S(1)}, u32[]{:S(2)}, u32[]{:S(2)}) %collective-permute-start.6) | collective-permute-done | bytes 1056 | tf_op jit(solution)/shard_map/ppermute | solution.py:308
  41.1 2.9 fusion.26
  44.8 2.6 collective-permute-start.13
  48.2 6.6 %shard_map.110 = bf16[256,512]{1,0:T(8,128)(2,1)} custom-call(bf16[128,5120]{1,0:T(8,128)(2,1)} %get-tuple-element.44.lo_ref, bf16[128,5120]{1,0:T(8,128)(2,1)} %get-tuple-element.43.hi_ref, f32[256,128]{1,0:T(8,128)} %pad_maximum_fusion.5.c_ref, f32[256,128]{1,0:T(8,128)} %pad_maximum_fusion.6.s_ref, bf16[5120,256]{1,0:T(8,128)(2,1)} %rest_0_.12, ...), custom_call_target="tpu_custom_call" | custom-call | flops 1342177280 | bytes 7864320 | tf_op jit(solution)/shard_map/pallas_call | solution.py:78
  54.8 2.9 collective-permute-start
  57.6 1.7 pad_maximum_fusion.11.c_ref
  59.4 1.7 pad_maximum_fusion.9.c_ref
  62.7 6.4 %collective-permute-done.19.lo_ref = bf16[128,5120]{1,0:T(8,128)(2,1)} collective-permute-done((bf16[128,5120]{1,0:T(8,128)(2,1)}, bf16[128,5120]{1,0:T(8,128)(2,1)}, u32[]{:S(2)}, u32[]{:S(2)}) %collective-permute-start.19) | collective-permute-done | bytes 1310752 | tf_op jit(solution)/shard_map/ppermute | solution.py:308
  69.1 3.0 collective-permute-start.1
  72.5 6.6 %shard_map.113 = bf16[256,512]{1,0:T(8,128)(2,1)} custom-call(bf16[128,5120]{1,0:T(8,128)(2,1)} %collective-permute-done.19.lo_ref, bf16[128,5120]{1,0:T(8,128)(2,1)} %collective-permute-done.20.hi_ref, f32[256,128]{1,0:T(8,128)} %pad_maximum_fusion.11.c_ref, f32[256,128]{1,0:T(8,128)} %pad_maximum_fusion.12.s_ref, bf16[5120,256]{1,0:T(8,128)(2,1)} %rest_0_.12, ...), custom_call_target="tpu_custom_call" | custom-call | flops 1342177280 | bytes 7864320 | tf_op jit(solution)/shard_map/pallas_call | solution.py:78
  79.1 2.2 collective-permute-start.21
  82.8 6.6 %shard_map.111 = bf16[256,512]{1,0:T(8,128)(2,1)} custom-call(bf16[128,5120]{1,0:T(8,128)(2,1)} %collective-permute-done.4.lo_ref, bf16[128,5120]{1,0:T(8,128)(2,1)} %collective-permute-done.5.hi_ref, f32[256,128]{1,0:T(8,128)} %pad_maximum_fusion.7.c_ref, f32[256,128]{1,0:T(8,128)} %pad_maximum_fusion.8.s_ref, bf16[5120,256]{1,0:T(8,128)(2,1)} %rest_0_.12, ...), custom_call_target="tpu_custom_call" | custom-call | flops 1342177280 | bytes 7864320 | tf_op jit(solution)/shard_map/pallas_call | solution.py:78
  90.7 1.6 collective-permute-start.10
  92.2 2.2 pad_maximum_fusion.1.rest_0_
  94.4 4.5 collective-permute-done.12.lo_ref
  99.0 2.9 collective-permute-start.8
  102.1 6.6 %shard_map.112 = bf16[256,512]{1,0:T(8,128)(2,1)} custom-call(bf16[128,5120]{1,0:T(8,128)(2,1)} %collective-permute-done.12.lo_ref, bf16[128,5120]{1,0:T(8,128)(2,1)} %collective-permute-done.13.hi_ref, f32[256,128]{1,0:T(8,128)} %pad_maximum_fusion.9.c_ref, f32[256,128]{1,0:T(8,128)} %pad_maximum_fusion.10.s_ref, bf16[5120,256]{1,0:T(8,128)(2,1)} %rest_0_.12, ...), custom_call_target="tpu_custom_call" | custom-call | flops 1342177280 | bytes 7864320 | tf_op jit(solution)/shard_map/pallas_call | solution.py:78
  109.5 2.1 collective-permute-start.16
  112.5 2.2 pad_maximum_fusion.4.rest_6_
  114.7 4.0 collective-permute-start.3
  119.3 2.1 pad_maximum_fusion.2.rest_2_
  121.4 4.0 collective-permute-start.11
  125.4 2.0 collective-permute-done.17
  129.0 9.9 %shard_map.109.q_ref = bf16[256,1280]{1,0:T(8,128)(2,1)} custom-call(bf16[128,5120]{1,0:T(8,128)(2,1)} %get-tuple-element.44.lo_ref, bf16[128,5120]{1,0:T(8,128)(2,1)} %get-tuple-element.43.hi_ref, f32[256,128]{1,0:T(8,128)} %pad_maximum_fusion.5.c_ref, f32[256,128]{1,0:T(8,128)} %pad_maximum_fusion.6.s_ref, bf16[5120,1280]{1,0:T(8,128)(2,1)} %rest_0_.15), custom_call_target="tpu_custom_call" | custom-call | flops 3355443200 | bytes 15728640 | tf_op jit(solution)/shard_map/pallas_call | solution.py:78
  138.9 9.9 %shard_map.117.q_ref = bf16[256,1280]{1,0:T(8,128)(2,1)} custom-call(bf16[128,5120]{1,0:T(8,128)(2,1)} %collective-permute-done.19.lo_ref, bf16[128,5120]{1,0:T(8,128)(2,1)} %collective-permute-done.20.hi_ref, f32[256,128]{1,0:T(8,128)} %pad_maximum_fusion.11.c_ref, f32[256,128]{1,0:T(8,128)} %pad_maximum_fusion.12.s_ref, bf16[5120,1280]{1,0:T(8,128)(2,1)} %rest_0_.15), custom_call_target="tpu_custom_call" | custom-call | flops 3355443200 | bytes 15728640 | tf_op jit(solution)/shard_map/pallas_call | solution.py:78
  148.8 9.9 %shard_map.115.q_ref = bf16[256,1280]{1,0:T(8,128)(2,1)} custom-call(bf16[128,5120]{1,0:T(8,128)(2,1)} %collective-permute-done.4.lo_ref, bf16[128,5120]{1,0:T(8,128)(2,1)} %collective-permute-done.5.hi_ref, f32[256,128]{1,0:T(8,128)} %pad_maximum_fusion.7.c_ref, f32[256,128]{1,0:T(8,128)} %pad_maximum_fusion.8.s_ref, bf16[5120,1280]{1,0:T(8,128)(2,1)} %rest_0_.15), custom_call_target="tpu_custom_call" | custom-call | flops 3355443200 | bytes 15728640 | tf_op jit(solution)/shard_map/pallas_call | solution.py:78
  158.6 9.9 %shard_map.119.q_ref = bf16[256,1280]{1,0:T(8,128)(2,1)} custom-call(bf16[128,5120]{1,0:T(8,128)(2,1)} %collective-permute-done.12.lo_ref, bf16[128,5120]{1,0:T(8,128)(2,1)} %collective-permute-done.13.hi_ref, f32[256,128]{1,0:T(8,128)} %pad_maximum_fusion.9.c_ref, f32[256,128]{1,0:T(8,128)} %pad_maximum_fusion.10.s_ref, bf16[5120,1280]{1,0:T(8,128)(2,1)} %rest_0_.15), custom_call_target="tpu_custom_call" | custom-call | flops 3355443200 | bytes 15728640 | tf_op jit(solution)/shard_map/pallas_call | solution.py:78
  168.5 27.0 %shard_map.120 = (bf16[128,5120]{1,0:T(8,128)(2,1)}, bf16[128,5120]{1,0:T(8,128)(2,1)}) custom-call(s32[2]{0:T(128)} %pad_add_fusion.info_ref, bf16[256,1280]{1,0:T(8,128)(2,1)} %shard_map.119.q_ref, bf16[1024,512]{1,0:T(8,128)(2,1)} %pad_maximum_fusion.1.rest_0_, bf16[1024,512]{1,0:T(8,128)(2,1)} %collective-permute-done.3.rest_1_, ...), custom_call_target="tpu_custom_call" | custom-call | flops 20000000000 | bytes 21495808 | tf_op jit(solution)/shard_map/pallas_call | solution.py:280
  195.7 27.1 %shard_map.116 = (bf16[128,5120]{1,0:T(8,128)(2,1)}, bf16[128,5120]{1,0:T(8,128)(2,1)}) custom-call(s32[2]{0:T(128)} %pad_add_fusion.info_ref, bf16[256,1280]{1,0:T(8,128)(2,1)} %shard_map.115.q_ref, bf16[1024,512]{1,0:T(8,128)(2,1)} %pad_maximum_fusion.1.rest_0_, bf16[1024,512]{1,0:T(8,128)(2,1)} %collective-permute-done.3.rest_1_, ...), custom_call_target="tpu_custom_call" | custom-call | flops 20000000000 | bytes 21495808 | tf_op jit(solution)/shard_map/pallas_call | solution.py:280
  222.7 2.7 collective-permute-start.25
  225.5 2.7 collective-permute-start.29
  228.1 27.9 %shard_map.118 = (f32[128,5120]{1,0:T(8,128)}, f32[128,5120]{1,0:T(8,128)}) custom-call(s32[2]{0:T(128)} %pad_add_fusion.info_ref, bf16[256,1280]{1,0:T(8,128)(2,1)} %shard_map.117.q_ref, bf16[1024,512]{1,0:T(8,128)(2,1)} %pad_maximum_fusion.1.rest_0_, bf16[1024,512]{1,0:T(8,128)(2,1)} %collective-permute-done.3.rest_1_, ...), custom_call_target="tpu_custom_call" | custom-call | flops 20000000000 | bytes 21495808 | tf_op jit(solution)/shard_map/pallas_call | solution.py:280
  256.0 3.6 add_convert_fusion.3
  259.6 22.1 %collective-permute-done.29 = bf16[128,5120]{1,0:T(8,128)(2,1)} collective-permute-done((bf16[128,5120]{1,0:T(8,128)(2,1)}, bf16[128,5120]{1,0:T(8,128)(2,1)}, u32[]{:S(2)}, u32[]{:S(2)}) %collective-permute-start.29) | collective-permute-done | bytes 1310752 | tf_op jit(solution)/shard_map/ppermute | solution.py:308
  281.7 2.7 add_convert_fusion.2
  284.4 3.4 collective-permute-start.30
  287.8 27.9 %shard_map.114 = (f32[128,5120]{1,0:T(8,128)}, f32[128,5120]{1,0:T(8,128)}) custom-call(s32[2]{0:T(128)} %pad_add_fusion.info_ref, bf16[256,1280]{1,0:T(8,128)(2,1)} %shard_map.109.q_ref, bf16[1024,512]{1,0:T(8,128)(2,1)} %pad_maximum_fusion.1.rest_0_, bf16[1024,512]{1,0:T(8,128)(2,1)} %collective-permute-done.3.rest_1_, ...), custom_call_target="tpu_custom_call" | custom-call | flops 20000000000 | bytes 21495808 | tf_op jit(solution)/shard_map/pallas_call | solution.py:280
  315.8 5.8 fusion.18
  323.1 2.8 collective-permute-start.34
  325.9 1.5 collective-permute-start.32
  327.8 31.4 %shard_map.121.a_ref = bf16[256,3456]{1,0:T(8,128)(2,1)} custom-call(bf16[128,5120]{1,0:T(8,128)(2,1)} %copy-done.6, bf16[128,5120]{1,0:T(8,128)(2,1)} %copy-done.5, bf16[5120,3456]{1,0:T(8,128)(2,1)} %w1_ref.7, bf16[5120,3456]{1,0:T(8,128)(2,1)} %w3_ref.7), custom_call_target="tpu_custom_call" | custom-call | flops 18119393280 | bytes 73400320 | tf_op jit(solution)/shard_map/pallas_call | solution.py:113
  359.2 20.9 %collective-permute-done.32.hi_ref = bf16[128,5120]{1,0:T(8,128)(2,1)} collective-permute-done((bf16[128,5120]{1,0:T(8,128)(2,1)S(1)}, bf16[128,5120]{1,0:T(8,128)(2,1)}, u32[]{:S(2)}, u32[]{:S(2)}) %collective-permute-start.32) | collective-permute-done | bytes 1310752 | tf_op jit(solution)/shard_map/ppermute | solution.py:308
  380.1 3.5 collective-permute-start.37
  383.6 31.3 %shard_map.123.a_ref = bf16[256,3456]{1,0:T(8,128)(2,1)} custom-call(bf16[128,5120]{1,0:T(8,128)(2,1)} %collective-permute-done.31.lo_ref, bf16[128,5120]{1,0:T(8,128)(2,1)} %collective-permute-done.32.hi_ref, bf16[5120,3456]{1,0:T(8,128)(2,1)} %w1_ref.7, bf16[5120,3456]{1,0:T(8,128)(2,1)} %w3_ref.7), custom_call_target="tpu_custom_call" | custom-call | flops 18119393280 | bytes 73400320 | tf_op jit(solution)/shard_map/pallas_call | solution.py:113
  414.9 19.1 %shard_map.124 = (bf16[128,5120]{1,0:T(8,128)(2,1)}, bf16[128,5120]{1,0:T(8,128)(2,1)}) custom-call(bf16[256,3456]{1,0:T(8,128)(2,1)} %shard_map.123.a_ref, bf16[3456,5120]{1,0:T(8,128)(2,1)} %w_ref.7), custom_call_target="tpu_custom_call" | custom-call | flops 9059696640 | bytes 37158912 | tf_op jit(solution)/shard_map/pallas_call | solution.py:137
  434.0 31.4 %shard_map.127.a_ref = bf16[256,3456]{1,0:T(8,128)(2,1)} custom-call(bf16[128,5120]{1,0:T(8,128)(2,1)} %collective-permute-done.36.lo_ref, bf16[128,5120]{1,0:T(8,128)(2,1)} %collective-permute-done.37.hi_ref, bf16[5120,3456]{1,0:T(8,128)(2,1)} %w1_ref.7, bf16[5120,3456]{1,0:T(8,128)(2,1)} %w3_ref.7), custom_call_target="tpu_custom_call" | custom-call | flops 18119393280 | bytes 73400320 | tf_op jit(solution)/shard_map/pallas_call | solution.py:113
  465.4 19.1 %shard_map.128 = (bf16[128,5120]{1,0:T(8,128)(2,1)}, bf16[128,5120]{1,0:T(8,128)(2,1)}) custom-call(bf16[256,3456]{1,0:T(8,128)(2,1)} %shard_map.127.a_ref, bf16[3456,5120]{1,0:T(8,128)(2,1)} %w_ref.7), custom_call_target="tpu_custom_call" | custom-call | flops 9059696640 | bytes 37158912 | tf_op jit(solution)/shard_map/pallas_call | solution.py:137
  484.5 1.6 collective-permute-start.38
  486.1 31.4 %shard_map.125.a_ref = bf16[256,3456]{1,0:T(8,128)(2,1)} custom-call(bf16[128,5120]{1,0:T(8,128)(2,1)} %collective-permute-done.34.lo_ref, bf16[128,5120]{1,0:T(8,128)(2,1)} %collective-permute-done.35.hi_ref, bf16[5120,3456]{1,0:T(8,128)(2,1)} %w1_ref.7, bf16[5120,3456]{1,0:T(8,128)(2,1)} %w3_ref.7), custom_call_target="tpu_custom_call" | custom-call | flops 18119393280 | bytes 73400320 | tf_op jit(solution)/shard_map/pallas_call | solution.py:113
  517.5 19.6 %shard_map.126 = (f32[128,5120]{1,0:T(8,128)}, f32[128,5120]{1,0:T(8,128)}) custom-call(bf16[256,3456]{1,0:T(8,128)(2,1)} %shard_map.125.a_ref, bf16[3456,5120]{1,0:T(8,128)(2,1)} %w_ref.7), custom_call_target="tpu_custom_call" | custom-call | flops 9059696640 | bytes 37158912 | tf_op jit(solution)/shard_map/pallas_call | solution.py:137
  538.3 3.4 add_convert_fusion.1
  542.0 19.8 %shard_map.122 = (f32[128,5120]{1,0:T(8,128)}, f32[128,5120]{1,0:T(8,128)}) custom-call(bf16[256,3456]{1,0:T(8,128)(2,1)} %shard_map.121.a_ref, bf16[3456,5120]{1,0:T(8,128)(2,1)} %w_ref.7), custom_call_target="tpu_custom_call" | custom-call | flops 9059696640 | bytes 37158912 | tf_op jit(solution)/shard_map/pallas_call | solution.py:137
  561.8 2.2 collective-permute-done.41
  564.0 1.7 add_convert_fusion
  565.7 2.3 collective-permute-start.42
  568.0 1.3 collective-permute-done.39
  569.4 2.6 fusion.17
  572.0 25.4 %collective-permute-done.40 = bf16[128,5120]{1,0:T(8,128)(2,1)S(1)} collective-permute-done((bf16[128,5120]{1,0:T(8,128)(2,1)}, bf16[128,5120]{1,0:T(8,128)(2,1)S(1)}, u32[]{:S(2)}, u32[]{:S(2)}) %collective-permute-start.40) | collective-permute-done | bytes 1310752 | tf_op jit(solution)/shard_map/ppermute | solution.py:308
  598.1 1.7 pad_maximum_fusion
  (114 shorter events, 18.4 us)
Async XLA Ops:
  0.0 3.2 copy-start
  3.2 7.5 %copy-start.17 = (s32[256]{0:T(256)S(1)}, s32[256]{0:T(256)}, u32[]{:S(2)}) copy-start(s32[256]{0:T(256)} %param.12) | copy-start | bytes 3076
  3.2 10.9 %copy-start.16 = (bf16[5120]{0:T(1024)(128)(2,1)S(1)}, bf16[5120]{0:T(1024)(128)(2,1)}, u32[]{:S(2)}) copy-start(bf16[5120]{0:T(1024)(128)(2,1)} %param.14) | copy-start | bytes 30724
  5.5 39.2 %collective-permute-start.4 = (bf16[128,5120]{1,0:T(8,128)(2,1)}, bf16[128,5120]{1,0:T(8,128)(2,1)}, u32[]{:S(2)}, u32[]{:S(2)}) collective-permute-start(bf16[128,5120]{1,0:T(8,128)(2,1)} %get-tuple-element.44.lo_ref), channel_id=1, source_target_pairs={{0,8},{8,16},{16,24},{24,0},{1,9},{9,17},{17,25},{25,1},{2,10},{10... | collective-permute-start | bytes 3932168 | tf_op jit(solution)/shard_map/ppermute | solution.py:308
  8.2 36.6 %collective-permute-start.5 = (bf16[128,5120]{1,0:T(8,128)(2,1)}, bf16[128,5120]{1,0:T(8,128)(2,1)}, u32[]{:S(2)}, u32[]{:S(2)}) collective-permute-start(bf16[128,5120]{1,0:T(8,128)(2,1)} %get-tuple-element.43.hi_ref), channel_id=1, source_target_pairs={{0,24},{8,0},{16,8},{24,16},{1,25},{9,1},{17,9},{25,17},{2,26},{10... | collective-permute-start | bytes 3932168 | tf_op jit(solution)/shard_map/ppermute | solution.py:308
  10.7 28.9 %collective-permute-start.6 = (s32[256]{0:T(256)S(1)}, s32[256]{0:T(256)S(1)}, u32[]{:S(2)}, u32[]{:S(2)}) collective-permute-start(s32[256]{0:T(256)S(1)} %copy-done.17), channel_id=1, source_target_pairs={{0,8},{8,16},{16,24},{24,0},{1,9},{9,17},{17,25},{25,1},{2,10},{10... | collective-permute-start | bytes 3080 | tf_op jit(solution)/shard_map/ppermute | solution.py:308
  10.7 30.4 %collective-permute-start.7 = (s32[256]{0:T(256)S(1)}, s32[256]{0:T(256)S(1)}, u32[]{:S(2)}, u32[]{:S(2)}) collective-permute-start(s32[256]{0:T(256)S(1)} %copy-done.17), channel_id=1, source_target_pairs={{0,24},{8,0},{16,8},{24,16},{1,25},{9,1},{17,9},{25,17},{2,26},{10... | collective-permute-start | bytes 3080 | tf_op jit(solution)/shard_map/ppermute | solution.py:308
  13.4 27.4 %collective-permute-start.14 = (s32[256]{0:T(256)S(1)}, s32[256]{0:T(256)S(1)}, u32[]{:S(2)}, u32[]{:S(2)}) collective-permute-start(s32[256]{0:T(256)S(1)} %copy-done.17), channel_id=1, source_target_pairs={{0,16},{8,24},{16,0},{24,8},{1,17},{9,25},{17,1},{25,9},{2,18},{10... | collective-permute-start | bytes 3080 | tf_op jit(solution)/shard_map/ppermute | solution.py:308
  39.6 29.5 %collective-permute-start.19 = (bf16[128,5120]{1,0:T(8,128)(2,1)}, bf16[128,5120]{1,0:T(8,128)(2,1)}, u32[]{:S(2)}, u32[]{:S(2)}) collective-permute-start(bf16[128,5120]{1,0:T(8,128)(2,1)} %get-tuple-element.44.lo_ref), channel_id=1, source_target_pairs={{0,24},{8,0},{16,8},{24,16},{1,25},{9,1},{17,9},{25,17},{2,26},{10... | collective-permute-start | bytes 3932168 | tf_op jit(solution)/shard_map/ppermute | solution.py:308
  40.8 31.3 %collective-permute-start.20 = (bf16[128,5120]{1,0:T(8,128)(2,1)}, bf16[128,5120]{1,0:T(8,128)(2,1)}, u32[]{:S(2)}, u32[]{:S(2)}) collective-permute-start(bf16[128,5120]{1,0:T(8,128)(2,1)} %get-tuple-element.43.hi_ref), channel_id=1, source_target_pairs={{0,8},{8,16},{16,24},{24,0},{1,9},{9,17},{17,25},{25,1},{2,10},{10... | collective-permute-start | bytes 3932168 | tf_op jit(solution)/shard_map/ppermute | solution.py:308
  44.7 54.2 %collective-permute-start.12 = (bf16[128,5120]{1,0:T(8,128)(2,1)}, bf16[128,5120]{1,0:T(8,128)(2,1)}, u32[]{:S(2)}, u32[]{:S(2)}) collective-permute-start(bf16[128,5120]{1,0:T(8,128)(2,1)} %collective-permute-done.4.lo_ref), channel_id=1, source_target_pairs={{0,8},{8,16},{16,24},{24,0},{1,9},{9,17},{17,25},{25,1},{2,10},{10... | collective-permute-start | bytes 3932168 | tf_op jit(solution)/shard_map/ppermute | solution.py:308
  44.8 57.1 %collective-permute-start.13 = (bf16[128,5120]{1,0:T(8,128)(2,1)}, bf16[128,5120]{1,0:T(8,128)(2,1)}, u32[]{:S(2)}, u32[]{:S(2)}) collective-permute-start(bf16[128,5120]{1,0:T(8,128)(2,1)} %collective-permute-done.5.hi_ref), channel_id=1, source_target_pairs={{0,24},{8,0},{16,8},{24,16},{1,25},{9,1},{17,9},{25,17},{2,26},{10... | collective-permute-start | bytes 3932168 | tf_op jit(solution)/shard_map/ppermute | solution.py:308
  54.8 24.3 %collective-permute-start = (bf16[256,512]{1,0:T(8,128)(2,1)}, bf16[256,512]{1,0:T(8,128)(2,1)}, u32[]{:S(2)}, u32[]{:S(2)}) collective-permute-start(bf16[256,512]{1,0:T(8,128)(2,1)} %shard_map.110), channel_id=1, source_target_pairs={{0,6},{1,7},{2,0},{3,1},{4,2},{5,3},{6,4},{7,5},{8,14},{9,15},{10,... | collective-permute-start | bytes 786440 | tf_op jit(solution)/shard_map/ppermute | solution.py:311
  69.1 20.4 %collective-permute-start.1 = (bf16[256,512]{1,0:T(8,128)(2,1)}, bf16[256,512]{1,0:T(8,128)(2,1)}, u32[]{:S(2)}, u32[]{:S(2)}) collective-permute-start(bf16[256,512]{1,0:T(8,128)(2,1)} %shard_map.110), channel_id=1, source_target_pairs={{0,4},{1,5},{2,6},{3,7},{4,0},{5,1},{6,2},{7,3},{8,12},{9,13},{10,... | collective-permute-start | bytes 786440 | tf_op jit(solution)/shard_map/ppermute | solution.py:311
  72.1 18.1 %collective-permute-start.2 = (bf16[256,512]{1,0:T(8,128)(2,1)}, bf16[256,512]{1,0:T(8,128)(2,1)}, u32[]{:S(2)}, u32[]{:S(2)}) collective-permute-start(bf16[256,512]{1,0:T(8,128)(2,1)} %shard_map.110), channel_id=1, source_target_pairs={{0,2},{1,3},{2,4},{3,5},{4,6},{5,7},{6,0},{7,1},{8,10},{9,11},{10,... | collective-permute-start | bytes 786440 | tf_op jit(solution)/shard_map/ppermute | solution.py:311
  79.1 11.5 %collective-permute-start.21 = (bf16[256,512]{1,0:T(8,128)(2,1)}, bf16[256,512]{1,0:T(8,128)(2,1)}, u32[]{:S(2)}, u32[]{:S(2)}) collective-permute-start(bf16[256,512]{1,0:T(8,128)(2,1)} %shard_map.113), channel_id=1, source_target_pairs={{0,6},{1,7},{2,0},{3,1},{4,2},{5,3},{6,4},{7,5},{8,14},{9,15},{10,... | collective-permute-start | bytes 786440 | tf_op jit(solution)/shard_map/ppermute | solution.py:311
  82.8 6.6 %copy-start.12 = (bf16[256,512]{1,0:T(8,128)(2,1)S(1)}, bf16[256,512]{1,0:T(8,128)(2,1)}, u32[]{:S(2)}) copy-start(bf16[256,512]{1,0:T(8,128)(2,1)} %shard_map.113) | copy-start | bytes 786436
  82.8 9.4 %copy-start.13 = (bf16[256,512]{1,0:T(8,128)(2,1)S(1)}, bf16[256,512]{1,0:T(8,128)(2,1)}, u32[]{:S(2)}) copy-start(bf16[256,512]{1,0:T(8,128)(2,1)} %shard_map.110) | copy-start | bytes 786436
  89.5 9.5 %copy-start.11 = (bf16[256,512]{1,0:T(8,128)(2,1)S(1)}, bf16[256,512]{1,0:T(8,128)(2,1)}, u32[]{:S(2)}) copy-start(bf16[256,512]{1,0:T(8,128)(2,1)} %shard_map.111) | copy-start | bytes 786436
  89.5 19.2 %collective-permute-start.22 = (bf16[256,512]{1,0:T(8,128)(2,1)S(1)}, bf16[256,512]{1,0:T(8,128)(2,1)}, u32[]{:S(2)}, u32[]{:S(2)}) collective-permute-start(bf16[256,512]{1,0:T(8,128)(2,1)S(1)} %copy-done.12), channel_id=1, source_target_pairs={{0,4},{1,5},{2,6},{3,7},{4,0},{5,1},{6,2},{7,3},{8,12},{9,13},{10,... | collective-permute-start | bytes 786440 | tf_op jit(solution)/shard_map/ppermute | solution.py:311
  90.2 19.3 %collective-permute-start.23 = (bf16[256,512]{1,0:T(8,128)(2,1)S(1)}, bf16[256,512]{1,0:T(8,128)(2,1)}, u32[]{:S(2)}, u32[]{:S(2)}) collective-permute-start(bf16[256,512]{1,0:T(8,128)(2,1)S(1)} %copy-done.12), channel_id=1, source_target_pairs={{0,2},{1,3},{2,4},{3,5},{4,6},{5,7},{6,0},{7,1},{8,10},{9,11},{10,... | collective-permute-start | bytes 786440 | tf_op jit(solution)/shard_map/ppermute | solution.py:311
  90.7 21.0 %collective-permute-start.10 = (bf16[256,512]{1,0:T(8,128)(2,1)}, bf16[256,512]{1,0:T(8,128)(2,1)}, u32[]{:S(2)}, u32[]{:S(2)}) collective-permute-start(bf16[256,512]{1,0:T(8,128)(2,1)} %shard_map.111), channel_id=1, source_target_pairs={{0,2},{1,3},{2,4},{3,5},{4,6},{5,7},{6,0},{7,1},{8,10},{9,11},{10,... | collective-permute-start | bytes 786440 | tf_op jit(solution)/shard_map/ppermute | solution.py:311
  99.0 15.7 %collective-permute-start.8 = (bf16[256,512]{1,0:T(8,128)(2,1)S(1)}, bf16[256,512]{1,0:T(8,128)(2,1)S(1)}, u32[]{:S(2)}, u32[]{:S(2)}) collective-permute-start(bf16[256,512]{1,0:T(8,128)(2,1)S(1)} %copy-done.11), channel_id=1, source_target_pairs={{0,6},{1,7},{2,0},{3,1},{4,2},{5,3},{6,4},{7,5},{8,14},{9,15},{10,... | collective-permute-start | bytes 786440 | tf_op jit(solution)/shard_map/ppermute | solution.py:311
  101.9 16.8 %collective-permute-start.9 = (bf16[256,512]{1,0:T(8,128)(2,1)S(1)}, bf16[256,512]{1,0:T(8,128)(2,1)}, u32[]{:S(2)}, u32[]{:S(2)}) collective-permute-start(bf16[256,512]{1,0:T(8,128)(2,1)S(1)} %copy-done.11), channel_id=1, source_target_pairs={{0,4},{1,5},{2,6},{3,7},{4,0},{5,1},{6,2},{7,3},{8,12},{9,13},{10,... | collective-permute-start | bytes 786440 | tf_op jit(solution)/shard_map/ppermute | solution.py:311
  108.7 18.7 %copy-start.14 = (bf16[256,512]{1,0:T(8,128)(2,1)S(1)}, bf16[256,512]{1,0:T(8,128)(2,1)}, u32[]{:S(2)}) copy-start(bf16[256,512]{1,0:T(8,128)(2,1)} %shard_map.112) | copy-start | bytes 786436
  108.7 12.7 %collective-permute-start.15 = (bf16[256,512]{1,0:T(8,128)(2,1)}, bf16[256,512]{1,0:T(8,128)(2,1)S(1)}, u32[]{:S(2)}, u32[]{:S(2)}) collective-permute-start(bf16[256,512]{1,0:T(8,128)(2,1)} %shard_map.112), channel_id=1, source_target_pairs={{0,6},{1,7},{2,0},{3,1},{4,2},{5,3},{6,4},{7,5},{8,14},{9,15},{10,... | collective-permute-start | bytes 786440 | tf_op jit(solution)/shard_map/ppermute | solution.py:311
  109.5 15.9 %collective-permute-start.16 = (bf16[256,512]{1,0:T(8,128)(2,1)}, bf16[256,512]{1,0:T(8,128)(2,1)S(1)}, u32[]{:S(2)}, u32[]{:S(2)}) collective-permute-start(bf16[256,512]{1,0:T(8,128)(2,1)} %shard_map.112), channel_id=1, source_target_pairs={{0,4},{1,5},{2,6},{3,7},{4,0},{5,1},{6,2},{7,3},{8,12},{9,13},{10,... | collective-permute-start | bytes 786440 | tf_op jit(solution)/shard_map/ppermute | solution.py:311
  111.6 15.7 %collective-permute-start.17 = (bf16[256,512]{1,0:T(8,128)(2,1)}, bf16[256,512]{1,0:T(8,128)(2,1)S(1)}, u32[]{:S(2)}, u32[]{:S(2)}) collective-permute-start(bf16[256,512]{1,0:T(8,128)(2,1)} %shard_map.112), channel_id=1, source_target_pairs={{0,2},{1,3},{2,4},{3,5},{4,6},{5,7},{6,0},{7,1},{8,10},{9,11},{10,... | collective-permute-start | bytes 786440 | tf_op jit(solution)/shard_map/ppermute | solution.py:311
  114.7 53.8 %collective-permute-start.3 = (bf16[1024,512]{1,0:T(8,128)(2,1)}, bf16[1024,512]{1,0:T(8,128)(2,1)}, u32[]{:S(2)}, u32[]{:S(2)}) collective-permute-start(bf16[1024,512]{1,0:T(8,128)(2,1)} %pad_maximum_fusion.1.rest_0_), channel_id=1, source_target_pairs={{0,1},{1,0},{2,3},{3,2},{4,5},{5,4},{6,7},{7,6},{8,9},{9,8},{10,11... | collective-permute-start | bytes 3145736 | tf_op jit(solution)/shard_map/ppermute | solution.py:314
  118.7 49.8 %collective-permute-start.24 = (bf16[1024,512]{1,0:T(8,128)(2,1)}, bf16[1024,512]{1,0:T(8,128)(2,1)}, u32[]{:S(2)}, u32[]{:S(2)}) collective-permute-start(bf16[1024,512]{1,0:T(8,128)(2,1)} %pad_maximum_fusion.4.rest_6_), channel_id=1, source_target_pairs={{0,1},{1,0},{2,3},{3,2},{4,5},{5,4},{6,7},{7,6},{8,9},{9,8},{10,11... | collective-permute-start | bytes 3145736 | tf_op jit(solution)/shard_map/ppermute | solution.py:314
  121.4 47.1 %collective-permute-start.11 = (bf16[1024,512]{1,0:T(8,128)(2,1)}, bf16[1024,512]{1,0:T(8,128)(2,1)}, u32[]{:S(2)}, u32[]{:S(2)}) collective-permute-start(bf16[1024,512]{1,0:T(8,128)(2,1)} %pad_maximum_fusion.2.rest_2_), channel_id=1, source_target_pairs={{0,1},{1,0},{2,3},{3,2},{4,5},{5,4},{6,7},{7,6},{8,9},{9,8},{10,11... | collective-permute-start | bytes 3145736 | tf_op jit(solution)/shard_map/ppermute | solution.py:314
  128.4 40.1 %collective-permute-start.18 = (bf16[1024,512]{1,0:T(8,128)(2,1)}, bf16[1024,512]{1,0:T(8,128)(2,1)}, u32[]{:S(2)}, u32[]{:S(2)}) collective-permute-start(bf16[1024,512]{1,0:T(8,128)(2,1)} %pad_maximum_fusion.3.rest_4_), channel_id=1, source_target_pairs={{0,1},{1,0},{2,3},{3,2},{4,5},{5,4},{6,7},{7,6},{8,9},{9,8},{10,11... | collective-permute-start | bytes 3145736 | tf_op jit(solution)/shard_map/ppermute | solution.py:314
  195.5 60.5 %collective-permute-start.26 = (bf16[128,5120]{1,0:T(8,128)(2,1)}, bf16[128,5120]{1,0:T(8,128)(2,1)}, u32[]{:S(2)}, u32[]{:S(2)}) collective-permute-start(bf16[128,5120]{1,0:T(8,128)(2,1)} %get-tuple-element.24), channel_id=1, source_target_pairs={{0,8},{8,16},{16,24},{24,0},{1,9},{9,17},{17,25},{25,1},{2,10},{10... | collective-permute-start | bytes 3932168 | tf_op jit(solution)/shard_map/ppermute | solution.py:308
  222.7 93.0 %collective-permute-start.25 = (bf16[128,5120]{1,0:T(8,128)(2,1)}, bf16[128,5120]{1,0:T(8,128)(2,1)}, u32[]{:S(2)}, u32[]{:S(2)}) collective-permute-start(bf16[128,5120]{1,0:T(8,128)(2,1)} %get-tuple-element.22), channel_id=1, source_target_pairs={{0,24},{8,0},{16,8},{24,16},{1,25},{9,1},{17,9},{25,17},{2,26},{10... | collective-permute-start | bytes 3932168 | tf_op jit(solution)/shard_map/ppermute | solution.py:308
  225.5 90.3 %collective-permute-start.28 = (bf16[128,5120]{1,0:T(8,128)(2,1)}, bf16[128,5120]{1,0:T(8,128)(2,1)}, u32[]{:S(2)}, u32[]{:S(2)}) collective-permute-start(bf16[128,5120]{1,0:T(8,128)(2,1)} %get-tuple-element.26), channel_id=1, source_target_pairs={{0,8},{8,16},{16,24},{24,0},{1,9},{9,17},{17,25},{25,1},{2,10},{10... | collective-permute-start | bytes 3932168 | tf_op jit(solution)/shard_map/ppermute | solution.py:308
  225.5 56.2 %collective-permute-start.29 = (bf16[128,5120]{1,0:T(8,128)(2,1)}, bf16[128,5120]{1,0:T(8,128)(2,1)}, u32[]{:S(2)}, u32[]{:S(2)}) collective-permute-start(bf16[128,5120]{1,0:T(8,128)(2,1)} %get-tuple-element.28), channel_id=1, source_target_pairs={{0,24},{8,0},{16,8},{24,16},{1,25},{9,1},{17,9},{25,17},{2,26},{10... | collective-permute-start | bytes 3932168 | tf_op jit(solution)/shard_map/ppermute | solution.py:308
  256.0 25.7 %copy-start.8 = (f32[128,5120]{1,0:T(8,128)S(1)}, f32[128,5120]{1,0:T(8,128)}, u32[]{:S(2)}) copy-start(f32[128,5120]{1,0:T(8,128)} %get-tuple-element.27) | copy-start | bytes 7864324
  259.6 56.1 %collective-permute-start.27 = (bf16[128,5120]{1,0:T(8,128)(2,1)}, bf16[128,5120]{1,0:T(8,128)(2,1)}, u32[]{:S(2)}, u32[]{:S(2)}) collective-permute-start(bf16[128,5120]{1,0:T(8,128)(2,1)} %add_convert_fusion.3), channel_id=1, source_target_pairs={{0,8},{8,16},{16,24},{24,0},{1,9},{9,17},{17,25},{25,1},{2,10},{10... | collective-permute-start | bytes 3932168 | tf_op jit(solution)/shard_map/ppermute | solution.py:308
  284.4 31.3 %collective-permute-start.30 = (bf16[128,5120]{1,0:T(8,128)(2,1)}, bf16[128,5120]{1,0:T(8,128)(2,1)}, u32[]{:S(2)}, u32[]{:S(2)}) collective-permute-start(bf16[128,5120]{1,0:T(8,128)(2,1)} %add_convert_fusion.2), channel_id=1, source_target_pairs={{0,24},{8,0},{16,8},{24,16},{1,25},{9,1},{17,9},{25,17},{2,26},{10... | collective-permute-start | bytes 3932168 | tf_op jit(solution)/shard_map/ppermute | solution.py:308
  315.7 5.8 copy-start.15
  321.5 1.2 copy-start.1
  321.5 1.6 copy-start.3
  323.1 4.7 copy-start.5
  323.1 4.7 copy-start.6
  323.1 36.1 %collective-permute-start.31 = (bf16[128,5120]{1,0:T(8,128)(2,1)S(1)}, bf16[128,5120]{1,0:T(8,128)(2,1)}, u32[]{:S(2)}, u32[]{:S(2)}) collective-permute-start(bf16[128,5120]{1,0:T(8,128)(2,1)S(1)} %get-tuple-element.48.lo_ref), channel_id=1, source_target_pairs={{0,8},{8,16},{16,24},{24,0},{1,9},{9,17},{17,25},{25,1},{2,10},{10... | collective-permute-start | bytes 3932168 | tf_op jit(solution)/shard_map/ppermute | solution.py:308
  323.1 163.0 %collective-permute-start.34 = (bf16[128,5120]{1,0:T(8,128)(2,1)S(1)}, bf16[128,5120]{1,0:T(8,128)(2,1)}, u32[]{:S(2)}, u32[]{:S(2)}) collective-permute-start(bf16[128,5120]{1,0:T(8,128)(2,1)S(1)} %get-tuple-element.48.lo_ref), channel_id=1, source_target_pairs={{0,24},{8,0},{16,8},{24,16},{1,25},{9,1},{17,9},{25,17},{2,26},{10... | collective-permute-start | bytes 3932168 | tf_op jit(solution)/shard_map/ppermute | solution.py:308
  325.9 54.2 %collective-permute-start.32 = (bf16[128,5120]{1,0:T(8,128)(2,1)S(1)}, bf16[128,5120]{1,0:T(8,128)(2,1)}, u32[]{:S(2)}, u32[]{:S(2)}) collective-permute-start(bf16[128,5120]{1,0:T(8,128)(2,1)S(1)} %get-tuple-element.47.hi_ref), channel_id=1, source_target_pairs={{0,24},{8,0},{16,8},{24,16},{1,25},{9,1},{17,9},{25,17},{2,26},{10... | collective-permute-start | bytes 3932168 | tf_op jit(solution)/shard_map/ppermute | solution.py:308
  327.3 158.7 %collective-permute-start.35 = (bf16[128,5120]{1,0:T(8,128)(2,1)S(1)}, bf16[128,5120]{1,0:T(8,128)(2,1)}, u32[]{:S(2)}, u32[]{:S(2)}) collective-permute-start(bf16[128,5120]{1,0:T(8,128)(2,1)S(1)} %get-tuple-element.47.hi_ref), channel_id=1, source_target_pairs={{0,8},{8,16},{16,24},{24,0},{1,9},{9,17},{17,25},{25,1},{2,10},{10... | collective-permute-start | bytes 3932168 | tf_op jit(solution)/shard_map/ppermute | solution.py:308
  359.2 74.9 %collective-permute-start.36 = (bf16[128,5120]{1,0:T(8,128)(2,1)}, bf16[128,5120]{1,0:T(8,128)(2,1)}, u32[]{:S(2)}, u32[]{:S(2)}) collective-permute-start(bf16[128,5120]{1,0:T(8,128)(2,1)} %collective-permute-done.31.lo_ref), channel_id=1, source_target_pairs={{0,8},{8,16},{16,24},{24,0},{1,9},{9,17},{17,25},{25,1},{2,10},{10... | collective-permute-start | bytes 3932168 | tf_op jit(solution)/shard_map/ppermute | solution.py:308
  380.1 54.0 %collective-permute-start.37 = (bf16[128,5120]{1,0:T(8,128)(2,1)}, bf16[128,5120]{1,0:T(8,128)(2,1)}, u32[]{:S(2)}, u32[]{:S(2)}) collective-permute-start(bf16[128,5120]{1,0:T(8,128)(2,1)} %collective-permute-done.32.hi_ref), channel_id=1, source_target_pairs={{0,24},{8,0},{16,8},{24,16},{1,25},{9,1},{17,9},{25,17},{2,26},{10... | collective-permute-start | bytes 3932168 | tf_op jit(solution)/shard_map/ppermute | solution.py:308
  434.0 134.0 %collective-permute-start.33 = (bf16[128,5120]{1,0:T(8,128)(2,1)}, bf16[128,5120]{1,0:T(8,128)(2,1)}, u32[]{:S(2)}, u32[]{:S(2)}) collective-permute-start(bf16[128,5120]{1,0:T(8,128)(2,1)} %get-tuple-element.30), channel_id=1, source_target_pairs={{0,24},{8,0},{16,8},{24,16},{1,25},{9,1},{17,9},{25,17},{2,26},{10... | collective-permute-start | bytes 3932168 | tf_op jit(solution)/shard_map/ppermute | solution.py:308
  484.5 53.9 %collective-permute-start.38 = (bf16[128,5120]{1,0:T(8,128)(2,1)}, bf16[128,5120]{1,0:T(8,128)(2,1)}, u32[]{:S(2)}, u32[]{:S(2)}) collective-permute-start(bf16[128,5120]{1,0:T(8,128)(2,1)} %get-tuple-element.32), channel_id=1, source_target_pairs={{0,8},{8,16},{16,24},{24,0},{1,9},{9,17},{17,25},{25,1},{2,10},{10... | collective-permute-start | bytes 3932168 | tf_op jit(solution)/shard_map/ppermute | solution.py:308
  537.1 26.9 %collective-permute-start.41 = (bf16[128,5120]{1,0:T(8,128)(2,1)}, bf16[128,5120]{1,0:T(8,128)(2,1)}, u32[]{:S(2)}, u32[]{:S(2)}) collective-permute-start(bf16[128,5120]{1,0:T(8,128)(2,1)} %get-tuple-element.36), channel_id=1, source_target_pairs={{0,24},{8,0},{16,8},{24,16},{1,25},{9,1},{17,9},{25,17},{2,26},{10... | collective-permute-start | bytes 3932168 | tf_op jit(solution)/shard_map/ppermute | solution.py:308
  541.8 22.3 %copy-start.7 = (f32[128,5120]{1,0:T(8,128)S(1)}, f32[128,5120]{1,0:T(8,128)}, u32[]{:S(2)}) copy-start(f32[128,5120]{1,0:T(8,128)} %get-tuple-element.35) | copy-start | bytes 7864324
  541.8 27.6 %collective-permute-start.39 = (bf16[128,5120]{1,0:T(8,128)(2,1)}, bf16[128,5120]{1,0:T(8,128)(2,1)}, u32[]{:S(2)}, u32[]{:S(2)}) collective-permute-start(bf16[128,5120]{1,0:T(8,128)(2,1)} %add_convert_fusion.1), channel_id=1, source_target_pairs={{0,8},{8,16},{16,24},{24,0},{1,9},{9,17},{17,25},{25,1},{2,10},{10... | collective-permute-start | bytes 3932168 | tf_op jit(solution)/shard_map/ppermute | solution.py:308
  561.8 35.6 %collective-permute-start.40 = (bf16[128,5120]{1,0:T(8,128)(2,1)}, bf16[128,5120]{1,0:T(8,128)(2,1)S(1)}, u32[]{:S(2)}, u32[]{:S(2)}) collective-permute-start(bf16[128,5120]{1,0:T(8,128)(2,1)} %get-tuple-element.34), channel_id=1, source_target_pairs={{0,8},{8,16},{16,24},{24,0},{1,9},{9,17},{17,25},{25,1},{2,10},{10... | collective-permute-start | bytes 3932168 | tf_op jit(solution)/shard_map/ppermute | solution.py:308
  564.0 5.4 copy-start.4
  564.0 5.4 copy-start.10
  565.7 31.6 %collective-permute-start.42 = (bf16[128,5120]{1,0:T(8,128)(2,1)S(1)}, bf16[128,5120]{1,0:T(8,128)(2,1)S(1)}, u32[]{:S(2)}, u32[]{:S(2)}) collective-permute-start(bf16[128,5120]{1,0:T(8,128)(2,1)S(1)} %add_convert_fusion), channel_id=1, source_target_pairs={{0,24},{8,0},{16,8},{24,16},{1,25},{9,1},{17,9},{25,17},{2,26},{10... | collective-permute-start | bytes 3932168 | tf_op jit(solution)/shard_map/ppermute | solution.py:308
  569.4 28.0 %copy-start.2 = (bf16[128,5120]{1,0:T(8,128)(2,1)S(1)}, bf16[128,5120]{1,0:T(8,128)(2,1)}, u32[]{:S(2)}) copy-start(bf16[128,5120]{1,0:T(8,128)(2,1)} %copy-done.1) | copy-start | bytes 3932164
  569.4 28.0 %copy-start.9 = (f32[128,5120]{1,0:T(8,128)S(1)}, f32[128,5120]{1,0:T(8,128)}, u32[]{:S(2)}) copy-start(f32[128,5120]{1,0:T(8,128)} %get-tuple-element.33) | copy-start | bytes 7864324
